TPU v7x, 512 devices: a whole 4x8x8 slice. The times are simulated.
512 devices in a mesh: blk: 8 (over x, z_hi), wide: 64 (over z_lo, y, core).
Axes of the slice: x: 4, y: 8, z: 8 (z_hi: 2, z_lo: 4; z = z_hi * 4 + z_lo), core: 2. Of those that a mesh axis runs over, the one named last changes fastest.
Arguments:
- volume: float32 [8, 2, 2048, 896], P('blk', None, 'wide'), may hold values from -1.6 to 1.6
- path_lengths: float32 [8, 8, 2], replicated, may hold values from 0.5 to 2
- probe: float32 [2, 128, 128], replicated, may hold values from -6 to 6
- measured: bfloat16 [8, 64, 14, 128, 128], P('blk', 'wide'), may hold values from 0.19921875 to 3
- jitter: int32 [2, 8, 64, 14], P(None, 'blk', 'wide'), may hold values from 0 to 15
- step_sizes: float32 [8], replicated, may hold values from 0.02 to 0.2
Outputs:
- new_volume: float32 [8, 2, 2048, 896], P('blk', None, 'wide')
- misfit: float32 [], replicated
All inputs are finite; a program needn't handle non-finite values.
Results may differ from a plain program's by a relative error of at most 0.0003.
Values sent between devices are 32-bit elements; how exact they have to be, the bound alone decides.
A program may use at most 64 MiB of HBM per device.

v0:
```python
import functools
import math

import jax
import jax.numpy as jnp
from jax import lax
from jax.sharding import Mesh
from jax.sharding import PartitionSpec as P

ROWS_DEV = 32
PATCH = 128
CSTEP = 64
BLK = ("blk_0", "blk_1")
WIDE = ("wide_0", "wide_1", "wide_2")
BLK_WIDE = ("blk_0", "blk_1", "wide_0", "wide_1", "wide_2")


highest = lax.Precision.HIGHEST
floor_value = 0.25


def in_blocks(shard, dim, count):
    dims = shard.shape
    parts = shard.reshape(*dims[:dim], count, dims[dim] // count, *dims[dim + 1 :])
    return jnp.moveaxis(parts, dim, 0)


def summed_on_arrival(shard, axis, dim):
    count = lax.axis_size(axis)
    parts = lax.all_to_all(in_blocks(shard, dim, count), axis, 0, 0, tiled=True)
    return jnp.sum(parts, axis=0)


def from_behind(shard, axis, by):
    count = lax.axis_size(axis)
    pairs = [(i, i + by) for i in range(count) if 0 <= i + by < count]
    return lax.ppermute(shard, axis, pairs)


def over_axes(shard, axes):
    return functools.reduce(lax.psum, axes, shard)


def from_everyone(shard, axis):
    count = lax.axis_size(axis)
    return lax.all_to_all(
        jnp.broadcast_to(shard[None], (count, *shard.shape)), axis, 0, 0, tiled=True
    )


def joined_along(parts, dim):
    parts = jnp.moveaxis(parts, 0, dim)
    dims = parts.shape
    return parts.reshape(*dims[:dim], dims[dim] * dims[dim + 1], *dims[dim + 2 :])


def gather_directly(shard, axis, dim):
    parts = from_everyone(shard, axis)
    return joined_along(parts, dim)


def dft_tables(length):
    grid = jnp.arange(length, dtype=jnp.int32)
    product = grid[:, None] * grid[None, :] % length
    angles = product.astype(jnp.float32) * (2.0 * math.pi / length)
    factor = 1.0 / math.sqrt(length)
    return (jnp.cos(angles) * factor, -jnp.sin(angles) * factor)


def left_apply(table, batch):
    return jnp.einsum("jk,bkl->bjl", table, batch, precision=highest)


def right_apply(batch, table):
    return jnp.einsum("bjk,kl->bjl", batch, table, precision=highest)


def transform(real_in, imag_in, cos_table, sin_table):
    mid_real = left_apply(cos_table, real_in) - left_apply(sin_table, imag_in)
    mid_imag = left_apply(cos_table, imag_in) + left_apply(sin_table, real_in)
    out_real = right_apply(mid_real, cos_table) - right_apply(mid_imag, sin_table)
    out_imag = right_apply(mid_real, sin_table) + right_apply(mid_imag, cos_table)
    return (out_real, out_imag)


def strip_update(
    strip_real,
    strip_imaginary,
    probe,
    measured,
    jitter_rows,
    jitter_cols,
    row_corner,
    column_corner,
):
    patch_len = probe.shape[-1]
    number = measured.shape[0]
    cos_table, sin_table = dft_tables(patch_len)
    starts_row = row_corner + jitter_rows
    starts_col = column_corner + CSTEP * jnp.arange(number, dtype=jnp.int32) + jitter_cols

    def window(image, top, left):
        return lax.dynamic_slice(image, (top, left), (patch_len, patch_len))

    pick = jax.vmap(window, in_axes=(None, 0, 0))
    obj_real = pick(strip_real, starts_row, starts_col)
    obj_imag = pick(strip_imaginary, starts_row, starts_col)
    probe_real = probe[0]
    probe_imag = probe[1]
    wave_real = probe_real * obj_real - probe_imag * obj_imag
    wave_imag = probe_real * obj_imag + probe_imag * obj_real
    far_real, far_imag = transform(wave_real, wave_imag, cos_table, sin_table)
    modulus = jnp.sqrt(far_real * far_real + far_imag * far_imag)
    target = measured.astype(jnp.float32)
    error = modulus - target
    partial_misfit = jnp.sum(error * error)
    ratio = target / jnp.maximum(modulus, floor_value)
    back_real, back_imag = transform(ratio * far_real, ratio * far_imag, cos_table, -sin_table)
    diff_real = back_real - wave_real
    diff_imag = back_imag - wave_imag
    corr_real = probe_real * diff_real + probe_imag * diff_imag
    corr_imag = probe_real * diff_imag - probe_imag * diff_real

    def place(position, sums):
        acc_real, acc_imag = sums
        top = starts_row[position]
        left = starts_col[position]
        acc_real = lax.dynamic_update_slice(
            acc_real, window(acc_real, top, left) + corr_real[position], (top, left)
        )
        acc_imag = lax.dynamic_update_slice(
            acc_imag, window(acc_imag, top, left) + corr_imag[position], (top, left)
        )
        return (acc_real, acc_imag)

    zeros = jnp.zeros(strip_real.shape, strip_real.dtype)
    acc_real, acc_imag = lax.fori_loop(0, number, place, (zeros, zeros))
    return (acc_real, acc_imag, partial_misfit)


def body(volume, path_lengths, probe, measured, jitter, step_sizes):
    group = lax.axis_index(BLK)
    column = lax.axis_index(WIDE)
    columns = lax.axis_size(WIDE)
    slab = volume[0]
    row_len = slab.shape[1]
    col_len = slab.shape[2]
    margin = probe.shape[-1] // 2
    own_paths = lax.dynamic_index_in_dim(path_lengths, group, 1, keepdims=False)
    angle_count = row_len * lax.axis_size(BLK) // row_len
    coeffs = own_paths
    terms = jnp.einsum("al,lrc->arc", coeffs, slab, precision=highest)
    projection = summed_on_arrival(terms.reshape(angle_count * row_len, col_len), BLK, 0)
    sources = (2, 1, 0, -1, -2)
    pieces_real = []
    pieces_imag = []
    for offset in sources:
        if offset == 0:
            got_phase = projection
        else:
            got_phase = from_behind(projection, WIDE, offset)
        source = column - offset
        valid = ((source >= 0) & (source < columns)).astype(jnp.float32)
        pieces_real.append(jnp.cos(got_phase) * valid)
        pieces_imag.append(jnp.sin(got_phase) * valid)
    ext_real = jnp.concatenate(pieces_real, 0)
    ext_imag = jnp.concatenate(pieces_imag, 0)
    strip_real = jnp.pad(ext_real, ((0, 0), (margin, margin)))
    strip_imaginary = jnp.pad(ext_imag, ((0, 0), (margin, margin)))
    row_corner = ROWS_DEV // 4
    column_corner = PATCH // 4 - ROWS_DEV // 4
    acc_real, acc_imag, local_misfit = strip_update(
        strip_real,
        strip_imaginary,
        probe,
        measured[0, 0],
        jitter[0, 0, 0],
        jitter[1, 0, 0],
        row_corner,
        column_corner,
    )
    acc_real = acc_real[:, margin : margin + col_len]
    acc_imag = acc_imag[:, margin : margin + col_len]

    def rows_of(array, slot):
        return array[slot * row_len : (slot + 1) * row_len]

    total_real = rows_of(acc_real, 2)
    total_imag = rows_of(acc_imag, 2)
    for offset in (-2, -1, 1, 2):
        got_real, got_imag = from_behind(
            (rows_of(acc_real, 2 + offset), rows_of(acc_imag, 2 + offset)), WIDE, offset
        )
        total_real = total_real + got_real
        total_imag = total_imag + got_imag
    gradient = rows_of(ext_real, 2) * total_imag - rows_of(ext_imag, 2) * total_real
    total_misfit = over_axes(local_misfit, BLK_WIDE)
    scaled = step_sizes[:, None] * own_paths
    coeffs = scaled
    update = jnp.einsum(
        "al,arc->lrc", coeffs, gather_directly(gradient[None], BLK, 0), precision=highest
    )
    return ((slab - update)[None], total_misfit)


def solution(mesh):
    split = Mesh(
        mesh.devices.reshape(4, 2, 4, 8, 2), ("blk_0", "blk_1", "wide_0", "wide_1", "wide_2")
    )
    in_specs = (
        P(BLK, None, WIDE, None),
        P(),
        P(),
        P(BLK, WIDE, None, None, None),
        P(None, BLK, WIDE, None),
        P(),
    )
    out_specs = (P(BLK, None, WIDE, None), P())
    return jax.shard_map(body, mesh=split, in_specs=in_specs, out_specs=out_specs, check_vma=False)
```

profile of v0, /device:TPU:1, one launch (start us, length us, event | category | flops | bytes accessed | tf_op | source)
XLA Modules:
  0.0 375.1 jit_solution(5032023670868648862)
XLA Ops:
  1.5 2.1 fusion.17
  4.7 13.4 %all-to-all-start = ((f32[8,32,896]{2,1,0:T(8,128)}), f32[8,32,896]{2,1,0:T(8,128)S(1)}, u32[]{:S(2)}, u32[]{:S(2)}) async-start(f32[8,32,896]{2,1,0:T(8,128)} %copy.52), calls=%async_computation | async-start | bytes 1835008 | tf_op jit(solution)/shard_map/all_to_all | solution.py:30
  18.2 17.2 %all-to-all-done = f32[8,32,896]{2,1,0:T(8,128)S(1)} async-done(((f32[8,32,896]{2,1,0:T(8,128)}), f32[8,32,896]{2,1,0:T(8,128)S(1)}, u32[]{:S(2)}, u32[]{:S(2)}) %all-to-all-start) | async-done | bytes 917536 | tf_op jit(solution)/shard_map/all_to_all | solution.py:30
  35.4 3.2 collective-permute-start
  38.7 5.4 %collective-permute-start.1 = (f32[32,896]{1,0:T(8,128)S(1)}, f32[32,896]{1,0:T(8,128)S(1)}, u32[]{:S(2)}, u32[]{:S(2)}) collective-permute-start(f32[32,896]{1,0:T(8,128)S(1)} %reduce_sum.18), channel_id=1, source_target_pairs={{0,1},{1,2},{2,3},{3,4},{4,5},{5,6},{6,7},{7,8},{8,9},{9,10},{10,1... | collective-permute-start | bytes 344072 | tf_op jit(solution)/shard_map/ppermute | solution.py:37
  53.3 28.5 %while.18 = (s32[]{:T(128)}, f32[160,1024]{1,0:T(8,128)S(1)}, s32[14,2]{0,1:T(2,128)S(1)}, f32[14,128,128]{2,1,0:T(8,128)S(1)}, s32[]{:T(128)}) while((s32[]{:T(128)}, f32[160,1024]{1,0:T(8,128)S(1)}, s32[14,2]{0,1:T(2,128)S(1)}, f32[14,128,128]{2,1,0:T(8,128)S(1)}, s32[]{:T(128)}) %tuple.85), condition=%wide.while_cond, body=%wide.while_body.sunk | while | flops 2 | bytes 131181 | solution.py:103
  82.1 28.7 %while.19 = (s32[]{:T(128)}, f32[160,1024]{1,0:T(8,128)S(1)}, s32[14,2]{0,1:T(2,128)S(1)}, f32[14,128,128]{2,1,0:T(8,128)S(1)}, s32[]{:T(128)}) while((s32[]{:T(128)}, f32[160,1024]{1,0:T(8,128)S(1)}, s32[14,2]{0,1:T(2,128)S(1)}, f32[14,128,128]{2,1,0:T(8,128)S(1)}, s32[]{:T(128)}) %tuple.91), condition=%wide.while_cond.1, body=%wide.while_body.1.sunk | while | flops 2 | bytes 131181 | solution.py:103
  123.6 2.5 fusion.8
  126.1 2.2 fusion.11
  128.3 2.2 fusion.15
  130.5 2.2 fusion.3
  136.5 2.2 fusion.2
  142.5 126.9 %while.17 = (s32[]{:T(128)}, f32[160,1024]{1,0:T(8,128)S(1)}, f32[160,1024]{1,0:T(8,128)S(1)}, s32[14]{0:T(128)S(1)}, s32[14]{0:T(128)S(1)}, /*index=5*/f32[14,1...) while((s32[]{:T(128)}, f32[160,1024]{1,0:T(8,128)S(1)}, ...), condition=%wide.region_2.3_spmd, body=%wide.region_1.2_spmd.sunk | while | flops 32776 | bytes 655581 | solution.py:137
  269.6 4.8 %collective-permute-start.10 = (f32[32,896]{1,0:T(8,128)S(1)}, f32[32,896]{1,0:T(8,128)S(1)}, u32[]{:S(2)}, u32[]{:S(2)}) collective-permute-start(f32[32,896]{1,0:T(8,128)S(1)} %get-tuple-element.197), channel_id=1, source_target_pairs={{0,1},{1,2},{2,3},{3,4},{4,5},{5,6},{6,7},{7,8},{8,9},{9,10},{10,1... | collective-permute-start | bytes 344072 | tf_op jit(solution)/shard_map/ppermute | solution.py:37
  274.4 3.3 collective-permute-start.11
  281.2 3.6 collective-permute-start.6
  284.8 4.9 %collective-permute-start.7 = (f32[32,896]{1,0:T(8,128)S(1)}, f32[32,896]{1,0:T(8,128)S(1)}, u32[]{:S(2)}, u32[]{:S(2)}) collective-permute-start(f32[32,896]{1,0:T(8,128)S(1)} %get-tuple-element.192), channel_id=1, source_target_pairs={{0,2},{1,3},{2,4},{3,5},{4,6},{5,7},{6,8},{7,9},{8,10},{9,11},{10,... | collective-permute-start | bytes 344072 | tf_op jit(solution)/shard_map/ppermute | solution.py:37
  293.0 3.1 collective-permute-done.8
  298.8 10.9 %all-to-all-start.1 = ((f32[8,1,32,896]{3,2,1,0:T(8,128)}), f32[8,1,32,896]{3,2,1,0:T(8,128)S(1)}, u32[]{:S(2)}, u32[]{:S(2)}) async-start(f32[8,1,32,896]{3,2,1,0:T(8,128)} %broadcast_in_dim.7), calls=%async_computation.1 | async-start | bytes 1835008 | tf_op jit(solution)/shard_map/all_to_all | solution.py:46
  309.7 10.9 %psum.35 = f32[]{:T(128)} all-reduce(f32[]{:T(128)} %get-tuple-element.213), channel_id=1, replica_groups=mesh['blk_0'=4,'blk_1'=2,'wide_0'=4,'wide_1'=8,'wide_2'=2] {'blk_0'}, use_global_device_ids=true, to_apply=%region_4.5 | all-reduce | flops 1 | bytes 8 | tf_op jit(solution)/shard_map/psum | solution.py:41
  320.6 16.5 %psum.36 = f32[]{:T(128)} all-reduce(f32[]{:T(128)} %psum.35), channel_id=1, replica_groups=mesh['blk_0'=4,'blk_1'=2,'wide_0'=4,'wide_1'=8,'wide_2'=2] {'blk_1'}, use_global_device_ids=true, to_apply=%region_5.6 | all-reduce | flops 1 | bytes 8 | tf_op jit(solution)/shard_map/psum | solution.py:41
  337.1 14.3 %psum.37 = f32[]{:T(128)} all-reduce(f32[]{:T(128)} %psum.36), channel_id=1, replica_groups=mesh['blk_0'=4,'blk_1'=2,'wide_0'=4,'wide_1'=8,'wide_2'=2] {'wide_0'}, use_global_device_ids=true, to_apply=%region_6.7 | all-reduce | flops 1 | bytes 8 | tf_op jit(solution)/shard_map/psum | solution.py:41
  351.4 11.6 %psum.38 = f32[]{:T(128)} all-reduce(f32[]{:T(128)} %psum.37), channel_id=1, replica_groups=mesh['blk_0'=4,'blk_1'=2,'wide_0'=4,'wide_1'=8,'wide_2'=2] {'wide_1'}, use_global_device_ids=true, to_apply=%region_7.8 | all-reduce | flops 1 | bytes 8 | tf_op jit(solution)/shard_map/psum | solution.py:41
  363.0 9.5 %psum.39 = f32[]{:T(128)} all-reduce(f32[]{:T(128)} %psum.38), channel_id=1, replica_groups=mesh['blk_0'=4,'blk_1'=2,'wide_0'=4,'wide_1'=8,'wide_2'=2] {'wide_2'}, use_global_device_ids=true, to_apply=%region_8.9 | all-reduce | flops 1 | bytes 8 | tf_op jit(solution)/shard_map/psum | solution.py:41
  (222 shorter events, 167.9 us)
Async XLA Ops:
  0.6 0.7 copy-start
  4.7 13.4 %copy-start.4 = (s32[2,1,1,14]{3,2,1,0:T(1,128)S(1)}, s32[2,1,1,14]{3,2,1,0:T(1,128)}, u32[]{:S(2)}) copy-start(s32[2,1,1,14]{3,2,1,0:T(1,128)} %param.12) | copy-start | bytes 340
  4.7 13.4 %copy-start.3 = (f32[2,128,128]{2,1,0:T(8,128)S(1)}, f32[2,128,128]{2,1,0:T(8,128)}, u32[]{:S(2)}) copy-start(f32[2,128,128]{2,1,0:T(8,128)} %param.10) | copy-start | bytes 393220
  4.7 30.7 %all-to-all-start = ((f32[8,32,896]{2,1,0:T(8,128)}), f32[8,32,896]{2,1,0:T(8,128)S(1)}, u32[]{:S(2)}, u32[]{:S(2)}) async-start(f32[8,32,896]{2,1,0:T(8,128)} %copy.52), calls=%async_computation | async-start | bytes 1835008 | tf_op jit(solution)/shard_map/all_to_all | solution.py:30
  35.4 11.9 %collective-permute-start = (f32[32,896]{1,0:T(8,128)S(1)}, f32[32,896]{1,0:T(8,128)S(1)}, u32[]{:S(2)}, u32[]{:S(2)}) collective-permute-start(f32[32,896]{1,0:T(8,128)S(1)} %reduce_sum.18), channel_id=1, source_target_pairs={{0,2},{1,3},{2,4},{3,5},{4,6},{5,7},{6,8},{7,9},{8,10},{9,11},{10,... | collective-permute-start | bytes 344072 | tf_op jit(solution)/shard_map/ppermute | solution.py:37
  38.7 9.1 %collective-permute-start.1 = (f32[32,896]{1,0:T(8,128)S(1)}, f32[32,896]{1,0:T(8,128)S(1)}, u32[]{:S(2)}, u32[]{:S(2)}) collective-permute-start(f32[32,896]{1,0:T(8,128)S(1)} %reduce_sum.18), channel_id=1, source_target_pairs={{0,1},{1,2},{2,3},{3,4},{4,5},{5,6},{6,7},{7,8},{8,9},{9,10},{10,1... | collective-permute-start | bytes 344072 | tf_op jit(solution)/shard_map/ppermute | solution.py:37
  44.1 6.1 %collective-permute-start.2 = (f32[32,896]{1,0:T(8,128)S(1)}, f32[32,896]{1,0:T(8,128)S(1)}, u32[]{:S(2)}, u32[]{:S(2)}) collective-permute-start(f32[32,896]{1,0:T(8,128)S(1)} %reduce_sum.18), channel_id=1, source_target_pairs={{1,0},{2,1},{3,2},{4,3},{5,4},{6,5},{7,6},{8,7},{9,8},{10,9},{11,1... | collective-permute-start | bytes 344072 | tf_op jit(solution)/shard_map/ppermute | solution.py:37
  46.0 6.5 %collective-permute-start.3 = (f32[32,896]{1,0:T(8,128)S(1)}, f32[32,896]{1,0:T(8,128)S(1)}, u32[]{:S(2)}, u32[]{:S(2)}) collective-permute-start(f32[32,896]{1,0:T(8,128)S(1)} %reduce_sum.18), channel_id=1, source_target_pairs={{2,0},{3,1},{4,2},{5,3},{6,4},{7,5},{8,6},{9,7},{10,8},{11,9},{12,... | collective-permute-start | bytes 344072 | tf_op jit(solution)/shard_map/ppermute | solution.py:37
  121.6 2.0 copy-start.2
  269.6 15.2 %collective-permute-start.10 = (f32[32,896]{1,0:T(8,128)S(1)}, f32[32,896]{1,0:T(8,128)S(1)}, u32[]{:S(2)}, u32[]{:S(2)}) collective-permute-start(f32[32,896]{1,0:T(8,128)S(1)} %get-tuple-element.197), channel_id=1, source_target_pairs={{0,1},{1,2},{2,3},{3,4},{4,5},{5,6},{6,7},{7,8},{8,9},{9,10},{10,1... | collective-permute-start | bytes 344072 | tf_op jit(solution)/shard_map/ppermute | solution.py:37
  274.4 15.4 %collective-permute-start.11 = (f32[32,896]{1,0:T(8,128)S(1)}, f32[32,896]{1,0:T(8,128)S(1)}, u32[]{:S(2)}, u32[]{:S(2)}) collective-permute-start(f32[32,896]{1,0:T(8,128)S(1)} %get-tuple-element.196), channel_id=1, source_target_pairs={{0,2},{1,3},{2,4},{3,5},{4,6},{5,7},{6,8},{7,9},{8,10},{9,11},{10,... | collective-permute-start | bytes 344072 | tf_op jit(solution)/shard_map/ppermute | solution.py:37
  277.9 13.1 %collective-permute-start.4 = (f32[32,896]{1,0:T(8,128)S(1)}, f32[32,896]{1,0:T(8,128)S(1)}, u32[]{:S(2)}, u32[]{:S(2)}) collective-permute-start(f32[32,896]{1,0:T(8,128)S(1)} %get-tuple-element.191), channel_id=1, source_target_pairs={{2,0},{3,1},{4,2},{5,3},{6,4},{7,5},{8,6},{9,7},{10,8},{11,9},{12,... | collective-permute-start | bytes 344072 | tf_op jit(solution)/shard_map/ppermute | solution.py:37
  279.2 13.8 %collective-permute-start.5 = (f32[32,896]{1,0:T(8,128)S(1)}, f32[32,896]{1,0:T(8,128)S(1)}, u32[]{:S(2)}, u32[]{:S(2)}) collective-permute-start(f32[32,896]{1,0:T(8,128)S(1)} %get-tuple-element.194), channel_id=1, source_target_pairs={{1,0},{2,1},{3,2},{4,3},{5,4},{6,5},{7,6},{8,7},{9,8},{10,9},{11,1... | collective-permute-start | bytes 344072 | tf_op jit(solution)/shard_map/ppermute | solution.py:37
  281.2 11.8 %collective-permute-start.6 = (f32[32,896]{1,0:T(8,128)S(1)}, f32[32,896]{1,0:T(8,128)S(1)}, u32[]{:S(2)}, u32[]{:S(2)}) collective-permute-start(f32[32,896]{1,0:T(8,128)S(1)} %get-tuple-element.193), channel_id=1, source_target_pairs={{0,1},{1,2},{2,3},{3,4},{4,5},{5,6},{6,7},{7,8},{8,9},{9,10},{10,1... | collective-permute-start | bytes 344072 | tf_op jit(solution)/shard_map/ppermute | solution.py:37
  284.8 8.2 %collective-permute-start.7 = (f32[32,896]{1,0:T(8,128)S(1)}, f32[32,896]{1,0:T(8,128)S(1)}, u32[]{:S(2)}, u32[]{:S(2)}) collective-permute-start(f32[32,896]{1,0:T(8,128)S(1)} %get-tuple-element.192), channel_id=1, source_target_pairs={{0,2},{1,3},{2,4},{3,5},{4,6},{5,7},{6,8},{7,9},{8,10},{9,11},{10,... | collective-permute-start | bytes 344072 | tf_op jit(solution)/shard_map/ppermute | solution.py:37
  289.8 6.4 %collective-permute-start.8 = (f32[32,896]{1,0:T(8,128)S(1)}, f32[32,896]{1,0:T(8,128)S(1)}, u32[]{:S(2)}, u32[]{:S(2)}) collective-permute-start(f32[32,896]{1,0:T(8,128)S(1)} %get-tuple-element.195), channel_id=1, source_target_pairs={{2,0},{3,1},{4,2},{5,3},{6,4},{7,5},{8,6},{9,7},{10,8},{11,9},{12,... | collective-permute-start | bytes 344072 | tf_op jit(solution)/shard_map/ppermute | solution.py:37
  291.1 6.2 %collective-permute-start.9 = (f32[32,896]{1,0:T(8,128)S(1)}, f32[32,896]{1,0:T(8,128)S(1)}, u32[]{:S(2)}, u32[]{:S(2)}) collective-permute-start(f32[32,896]{1,0:T(8,128)S(1)} %get-tuple-element.198), channel_id=1, source_target_pairs={{1,0},{2,1},{3,2},{4,3},{5,4},{6,5},{7,6},{8,7},{9,8},{10,9},{11,1... | collective-permute-start | bytes 344072 | tf_op jit(solution)/shard_map/ppermute | solution.py:37
  298.8 73.7 %copy-start.1 = (f32[1,2,32,896]{3,2,1,0:T(8,128)S(1)}, f32[1,2,32,896]{3,2,1,0:T(8,128)}, u32[]{:S(2)}) copy-start(f32[1,2,32,896]{3,2,1,0:T(8,128)} %param.8) | copy-start | bytes 688132
  298.8 73.7 %all-to-all-start.1 = ((f32[8,1,32,896]{3,2,1,0:T(8,128)}), f32[8,1,32,896]{3,2,1,0:T(8,128)S(1)}, u32[]{:S(2)}, u32[]{:S(2)}) async-start(f32[8,1,32,896]{3,2,1,0:T(8,128)} %broadcast_in_dim.7), calls=%async_computation.1 | async-start | bytes 1835008 | tf_op jit(solution)/shard_map/all_to_all | solution.py:46
  363.0 9.5 %copy-start.5 = (f32[8]{0:T(128)S(1)}, f32[8]{0:T(128)}, u32[]{:S(2)}) copy-start(f32[8]{0:T(128)} %param.13) | copy-start | bytes 100
where the time goes:
time: 381 us; the launch traced here: 375 us
  local copies, waits for them, and re-layouts  128 us (34%)
  blocking collectives  62.8 us (16%)
  loops' own time  59.5 us (16%)
  starting transfers between devices  59.3 us (16%)
  matrix products  34.6 us (9%)
  waiting for transfers between devices  25 us (7%)
  other arithmetic  4.58 us (1%)
    psum x5, blocking collectives, over_axes(): return functools.reduce(lax.psum, axes, shard)  62.8 us
    another operation x1, loops' own time, strip_update(): acc_real, acc_imag = lax.fori_loop(0, number, place, (zeros, zeros))  58.7 us
    gather x84, local copies, waits for them, and re-layouts  56.4 us
    ppermute x12, starting transfers between devices, from_behind(): return lax.ppermute(shard, axis, pairs)  34.9 us
    dynamic_update_slice x14, local copies, waits for them, and re-layouts, place(): lax.dynamic_update_slice(acc_imag, window(acc_imag, top, left) + corr_ima...  24 us
    dynamic_update_slice x14, local copies, waits for them, and re-layouts, place(): lax.dynamic_update_slice(acc_real, window(acc_real, top, left) + corr_rea...  24 us
    all_to_all x1, waiting for transfers between devices, summed_on_arrival(): parts = lax.all_to_all(in_blocks(shard, dim, count), axis, 0, 0, tiled=True)  17.2 us
    dot_general x8, matrix products, left_apply(): return jnp.einsum('jk,bkl->bjl', table, batch, precision=highest)  15.7 us
  transfers between devices with their start and end apart: 14, of which 5 were waited for; matrix products, arithmetic and copies ran while one was open for 1% of the time, Pallas kernels for 0%

commit v1 on v0

v1 whole, which is shorter than its diff:
```python
import functools

import jax
import jax.numpy as jnp
import ml_dtypes
import numpy as np
from jax import lax
from jax.experimental import pallas as pl
from jax.experimental.pallas import tpu as pltpu
from jax.sharding import PartitionSpec as P

ROWS = 32
COLS = 896
PATCH = 128
PCOLS = 14
N_BLK = 8
N_WIDE = 64
TILES = COLS // 128
FRAME = 144
TOP = 56
CHUNK = 32
F32 = jnp.float32
BF16 = jnp.bfloat16


def dft_tables():
    n = np.arange(PATCH)
    angle = (n[:, None] * n[None, :] % PATCH) * (2 * np.pi / PATCH)
    c = np.cos(angle) / np.sqrt(float(PATCH))
    s = -np.sin(angle) / np.sqrt(float(PATCH))
    out = []
    for t in (np.block([[c, s], [-s, c]]), np.block([[c, -s], [s, c]])):
        t = t.astype(np.float32)
        hi = t.astype(ml_dtypes.bfloat16)
        out += [hi, (t - hi.astype(np.float32)).astype(ml_dtypes.bfloat16)]
    return np.stack(out)


def cos_sin(x):
    k = jnp.floor(x * np.float32(2 / np.pi) + np.float32(0.5))
    r = x - k * np.float32(1.5703125)
    r = r - k * np.float32(4.837512969970703125e-4)
    r = r - k * np.float32(7.54978995489188216e-8)
    z = r * r
    sn = ((np.float32(-1.9515295891e-4) * z + np.float32(8.3321608736e-3)) * z - np.float32(1.6666654611e-1)) * z * r + r
    cs = ((np.float32(2.443315711809948e-5) * z - np.float32(1.388731625493765e-3)) * z + np.float32(4.166664568298827e-2)) * z * z
    cs = cs - np.float32(0.5) * z + np.float32(1.0)
    q = k.astype(jnp.int32)
    swap = (q & 1) == 1
    co = jnp.where(swap, sn, cs)
    si = jnp.where(swap, cs, sn)
    co = jnp.where(((q + 1) & 2) == 2, -co, co)
    si = jnp.where((q & 2) == 2, -si, si)
    return co, si


def halves(x):
    hi = x.astype(BF16)
    return hi, (x - hi.astype(F32)).astype(BF16)


def mm(a, b):
    return jnp.dot(a, b, preferred_element_type=F32)


def row_chunks():
    return [pl.ds(r, CHUNK) for r in range(0, PATCH, CHUNK)]


def mid_kernel(phase, probe, measured, jitter, tables, grad, misfit, cosf, sinf, acc, probe2, wave, xs, vs, err):
    w = lax.axis_index("wide")
    probe2[:, :PATCH] = probe[...]
    probe2[:, PATCH:] = probe[...]
    first = TOP - ROWS * w
    for r in range(0, FRAME, 16):
        row = lax.broadcasted_iota(jnp.int32, (16, COLS), 0) + r
        inside = (row >= first) & (row < first + ROWS * N_WIDE)
        co, si = cos_sin(phase[r : r + 16, :])
        co = jnp.where(inside, co, 0.0)
        si = jnp.where(inside, si, 0.0)
        for t in range(TILES):
            cosf[t + 1, r : r + 16, :] = co[:, t * 128 : t * 128 + 128]
            sinf[t + 1, r : r + 16, :] = si[:, t * 128 : t * 128 + 128]
    for t in (0, TILES + 1):
        cosf[t] = jnp.zeros((FRAME, 128), F32)
        sinf[t] = jnp.zeros((FRAME, 128), F32)
    acc[...] = jnp.zeros(acc.shape, F32)
    err[...] = jnp.zeros(err.shape, F32)

    def masks(pair, p):
        j = 2 * pair + p
        jr = jitter[0, j]
        s = (24 if p else 88) + jitter[1, j]
        lane = lax.broadcasted_iota(jnp.int32, (CHUNK, PATCH), 1) >= s
        row = lax.broadcasted_iota(jnp.int32, (16, PATCH), 0) >= jr
        return j, jr, s, lane, row

    def step(pair, slot):
        t1h, t1l, t2h, t2l = (tables[i] for i in range(4))
        for p in range(2):
            j, jr, s, lane, row = masks(pair, p)
            t = pair + p
            for c in range(0, PATCH, CHUNK):
                def pick(ref):
                    a = ref[t, c : c + CHUNK, :]
                    b = ref[t + 1, c : c + CHUNK, :]
                    if c == 0:
                        a0 = jnp.where(row, a[:16], ref[t, PATCH:, :])
                        b0 = jnp.where(row, b[:16], ref[t + 1, PATCH:, :])
                        a = jnp.concatenate([a0, a[16:]], 0)
                        b = jnp.concatenate([b0, b[16:]], 0)
                    return jnp.where(lane, a, b)
                o_r, o_i = pick(cosf), pick(sinf)
                at = pl.ds(PATCH - jr + c, CHUNK)
                p_r = pltpu.roll(probe2[0, at, :], s, 1)
                p_i = pltpu.roll(probe2[1, at, :], s, 1)
                w_r = p_r * o_r - p_i * o_i
                w_i = p_r * o_i + p_i * o_r
                wave[slot, p, 0, c : c + CHUNK, :] = w_r
                wave[slot, p, 1, c : c + CHUNK, :] = w_i
                put_rows(slot, p, c, w_r, w_i)
        right_to_cols(slot, t1h, t1l)
        y = left(slot, t2h, t2l)
        e = err[...]
        for p in range(2):
            j = 2 * pair + p
            for c in range(0, PATCH, CHUNK):
                f_r = y[c : c + CHUNK, p * 128 : p * 128 + 128]
                f_i = y[PATCH + c : PATCH + c + CHUNK, p * 128 : p * 128 + 128]
                m2 = f_r * f_r + f_i * f_i
                target = measured[j, c : c + CHUNK, :].astype(F32)
                d = jnp.sqrt(m2) - target
                d2 = d * d
                for k in range(0, CHUNK, 8):
                    e = e + d2[k : k + 8]
                ratio = target * lax.rsqrt(jnp.maximum(m2, 0.0625))
                put_rows(slot, p, c, ratio * f_r, ratio * f_i)
        err[...] = e
        right_to_cols(slot, t2h, t2l)
        y = left(slot, t1h, t1l)
        for p in range(2):
            j, jr, s, lane, row = masks(pair, p)
            t = pair + p
            for c in range(0, PATCH, CHUNK):
                b_r = y[c : c + CHUNK, p * 128 : p * 128 + 128]
                b_i = y[PATCH + c : PATCH + c + CHUNK, p * 128 : p * 128 + 128]
                g = wave[slot, p, 0, c : c + CHUNK, :] * b_i - wave[slot, p, 1, c : c + CHUNK, :] * b_r
                for tile, part in ((t, jnp.where(lane, g, 0.0)), (t + 1, jnp.where(lane, 0.0, g))):
                    if c == 0:
                        acc[tile, PATCH:, :] += jnp.where(row, 0.0, part[:16])
                        part = jnp.concatenate([jnp.where(row, part[:16], 0.0), part[16:]], 0)
                    acc[tile, c : c + CHUNK, :] += part

    def put_rows(slot, p, c, a, b):
        at = slice(p * PATCH + c, p * PATCH + c + CHUNK)
        for k, x in enumerate((a, b)):
            hi, lo = halves(x)
            xs[slot, at, k * 128 : k * 128 + 128] = hi
            xs[slot, at, 256 + k * 128 : 256 + k * 128 + 128] = lo

    def right_to_cols(slot, th, tl):
        x = xs[slot]
        u = mm(jnp.concatenate([x, x[:, :256]], 1), jnp.concatenate([th, th, tl], 0))
        for p in range(2):
            for k in range(2):
                for c in range(0, PATCH, CHUNK):
                    hi, lo = halves(u[p * PATCH + c : p * PATCH + c + CHUNK, k * 128 : k * 128 + 128])
                    vs[slot, k * PATCH + c : k * PATCH + c + CHUNK, p * 128 : p * 128 + 128] = hi
                    vs[slot, 256 + k * PATCH + c : 256 + k * PATCH + c + CHUNK, p * 128 : p * 128 + 128] = lo

    def left(slot, th, tl):
        v = vs[slot]
        return mm(jnp.concatenate([th, th, tl], 1), jnp.concatenate([v, v[:256]], 0))

    SLOTS = xs.shape[0]
    if SLOTS == PCOLS // 2:
        for pair in range(PCOLS // 2):
            step(pair, pair)
    else:
        def loop(i, carry):
            step(i, 0)
            return carry
        lax.fori_loop(0, PCOLS // 2, loop, 0)
    for t in range(TILES):
        grad[:, t * 128 : t * 128 + 128] = acc[t + 1]
    misfit[...] = err[...]


def middle(phase, probe, measured, jitter, slots=7):
    vm = pl.BlockSpec(memory_space=pltpu.VMEM)
    return pl.pallas_call(
        mid_kernel,
        out_shape=(jax.ShapeDtypeStruct((FRAME, COLS), F32), jax.ShapeDtypeStruct((8, 128), F32)),
        in_specs=[vm, vm, vm, pl.BlockSpec(memory_space=pltpu.SMEM), vm],
        out_specs=(vm, vm),
        scratch_shapes=[
            pltpu.VMEM((TILES + 2, FRAME, 128), F32),
            pltpu.VMEM((TILES + 2, FRAME, 128), F32),
            pltpu.VMEM((TILES + 2, FRAME, 128), F32),
            pltpu.VMEM((2, 2 * PATCH, PATCH), F32),
            pltpu.VMEM((slots, 2, 2, PATCH, PATCH), F32),
            pltpu.VMEM((slots, 2 * PATCH, 512), BF16),
            pltpu.VMEM((slots, 512, 2 * PATCH), BF16),
            pltpu.VMEM((8, 128), F32),
        ],
        name="middle",
    )(phase, probe, measured, jitter, jnp.asarray(dft_tables()))


def shifted(x, by):
    pairs = [(i, i + by) for i in range(N_WIDE) if 0 <= i + by < N_WIDE]
    return lax.ppermute(x, "wide", pairs)


def body(volume, path_lengths, probe, measured, jitter, step_sizes):
    group = lax.axis_index("blk")
    slab = volume[0]
    own = lax.dynamic_index_in_dim(path_lengths, group, 1, keepdims=False)
    terms = own[:, 0, None, None] * slab[0] + own[:, 1, None, None] * slab[1]
    proj = jnp.sum(lax.all_to_all(terms, "blk", 0, 0, tiled=True), 0)
    frame = jnp.concatenate(
        [shifted(proj[8:], 2), shifted(proj, 1), proj, shifted(proj, -1), shifted(proj[:24], -2)], 0
    )
    part, err = middle(frame, probe, measured[0, 0], jitter[:, 0, 0])
    grad = part[56:88]
    grad = grad + shifted(part[24:56], -1) + shifted(part[88:120], 1)
    grad = grad + jnp.pad(shifted(part[:24], -2), ((8, 0), (0, 0))) + jnp.pad(shifted(part[120:], 2), ((0, 8), (0, 0)))
    total = lax.psum(jnp.sum(err), ("blk", "wide"))
    every = lax.all_to_all(jnp.broadcast_to(grad[None], (N_BLK, ROWS, COLS)), "blk", 0, 0, tiled=True)
    coeffs = step_sizes[:, None] * own
    update = jnp.sum(coeffs[:, :, None, None] * every[:, None], 0)
    return (slab - update)[None], total


def solution(mesh):
    in_specs = (
        P("blk", None, "wide", None),
        P(),
        P(),
        P("blk", "wide", None, None, None),
        P(None, "blk", "wide", None),
        P(),
    )
    out_specs = (P("blk", None, "wide", None), P())
    return jax.shard_map(body, mesh=mesh, in_specs=in_specs, out_specs=out_specs, check_vma=False)
```

time: 381 us -> 210 us (0.55); the launches traced: 375 us -> 209 us
  local copies, waits for them, and re-layouts: 128 us -> 5.71 us
  blocking collectives: 62.8 us -> 149 us
  loops' own time: 59.5 us -> 0 us
  matrix products: 34.6 us -> 0 us
  starting transfers between devices: 59.3 us -> 34 us
  waiting for transfers between devices: 25 us -> 6.35 us
  Pallas kernels: 0 us -> 10 us
    another operation x3 -> x0, loops' own time: 59.5 us -> none  [the longest x1 58.7 us: strip_update(): acc_real, acc_imag = lax.fori_loop(0, number, place, (zeros, zeros))]
    gather x84 -> x0, local copies, waits for them, and re-layouts: 56.4 us -> none
    psum x5 -> x1, blocking collectives: 62.8 us -> 119 us  [body(): total = lax.psum(jnp.sum(err), ('blk', 'wide'))]
    dynamic_update_slice x28 -> x0, local copies, waits for them, and re-layouts: 47.9 us -> none  [the longest x14 24 us: place(): lax.dynamic_update_slice(acc_imag, window(acc_imag, top, left) + corr_ima...]
    dot_general x18 -> x0, matrix products: 34.6 us -> none  [the longest x8 15.7 us: left_apply(): return jnp.einsum('jk,bkl->bjl', table, batch, precision=highest)]
    all_to_all x0 -> x1, blocking collectives: none -> 30.7 us  [body(): proj = jnp.sum(lax.all_to_all(terms, 'blk', 0, 0, tiled=True), 0)]
    dynamic_slice x29 -> x2, local copies, waits for them, and re-layouts: 18.7 us -> 0.17 us  [body(): own = lax.dynamic_index_in_dim(path_lengths, group, 1, keepdims=False)]
    all_to_all x2 -> x1, waiting for transfers between devices: 17.2 us -> 0.01 us  [body(): lax.all_to_all(jnp.broadcast_to(grad[None], (N_BLK, ROWS, COLS)), 'blk',...]
  transfers between devices with their start and end apart: 14 -> 9, of which waited for: 5 -> 4; matrix products, arithmetic and copies ran while one was open for 1% -> 1% of each run, Pallas kernels for 0% -> 0%
where the time goes in v1:
time: 210 us; the launch traced here: 209 us
  blocking collectives  149 us (71%)
  starting transfers between devices  34 us (16%)
  Pallas kernels  10 us (5%)
  waiting for transfers between devices  6.35 us (3%)
  local copies, waits for them, and re-layouts  5.71 us (3%)
  other arithmetic  2.67 us (1%)
    psum x1, blocking collectives, body(): total = lax.psum(jnp.sum(err), ('blk', 'wide'))  119 us
    all_to_all x1, blocking collectives, body(): proj = jnp.sum(lax.all_to_all(terms, 'blk', 0, 0, tiled=True), 0)  30.7 us
    ppermute x8, starting transfers between devices, shifted(): return lax.ppermute(x, 'wide', pairs)  23.9 us
    all_to_all x1, starting transfers between devices, body(): lax.all_to_all(jnp.broadcast_to(grad[None], (N_BLK, ROWS, COLS)), 'blk',...  10.1 us
    pallas_call x1, Pallas kernels, middle(): pl.pallas_call(mid_kernel, out_shape=(jax.ShapeDtypeStruct((FRAME, COLS),...  10 us
    ppermute x8, waiting for transfers between devices, shifted(): return lax.ppermute(x, 'wide', pairs)  6.35 us
  transfers between devices with their start and end apart: 9, of which 4 were waited for; matrix products, arithmetic and copies ran while one was open for 1% of the time, Pallas kernels for 0%

profile of v1, /device:TPU:1, one launch (start us, length us, event | category | flops | bytes accessed | tf_op | source)
XLA Modules:
  0.0 209.0 jit_solution(15194638153656180084)
XLA Ops:
  0.6 0.7 copy-done
  1.5 1.0 slice_bitcast_fusion.1
  2.7 30.7 %all_to_all.10 = f32[8,32,896]{2,1,0:T(8,128)S(1)} all-to-all(f32[8,32,896]{2,1,0:T(8,128)S(1)} %multiply_add_fusion), channel_id=1, replica_groups=mesh['blk'=8,'wide'=64] {'blk'}, dimensions={0} | all-to-all | bytes 1835008 | tf_op jit(solution)/shard_map/all_to_all | solution.py:220
  33.4 3.2 %collective-permute-start = (f32[24,896]{1,0:T(8,128)S(1)}, f32[24,896]{1,0:T(8,128)S(1)}, u32[]{:S(2)}, u32[]{:S(2)}) collective-permute-start(f32[24,896]{1,0:T(8,128)S(1)} %get-tuple-element.13), channel_id=1, source_target_pairs={{0,2},{1,3},{2,4},{3,5},{4,6},{5,7},{6,8},{7,9},{8,10},{9,11},{10,... | collective-permute-start | bytes 258056 | tf_op jit(solution)/shard_map/ppermute | solution.py:212
  36.6 5.2 %collective-permute-start.1 = (f32[32,896]{1,0:T(8,128)S(1)}, f32[32,896]{1,0:T(8,128)S(1)}, u32[]{:S(2)}, u32[]{:S(2)}) collective-permute-start(f32[32,896]{1,0:T(8,128)S(1)} %reduce_sum.29), channel_id=1, source_target_pairs={{0,1},{1,2},{2,3},{3,4},{4,5},{5,6},{6,7},{7,8},{8,9},{9,10},{10,1... | collective-permute-start | bytes 344072 | tf_op jit(solution)/shard_map/ppermute | solution.py:212
  41.8 1.9 collective-permute-start.2
  43.8 1.3 collective-permute-start.3
  45.1 2.8 %collective-permute-done.2 = f32[32,896]{1,0:T(8,128)S(1)} collective-permute-done((f32[32,896]{1,0:T(8,128)S(1)}, f32[32,896]{1,0:T(8,128)S(1)}, u32[]{:S(2)}, u32[]{:S(2)}) %collective-permute-start.2) | collective-permute-done | bytes 114720 | tf_op jit(solution)/shard_map/ppermute | solution.py:212
  48.0 1.7 collective-permute-done.3
  49.6 0.8 copy-done.2
  50.4 10.0 %middle.1 = (f32[144,896]{1,0:T(8,128)}, f32[8,128]{1,0:T(8,128)}) custom-call(f32[144,896]{1,0:T(8,128)} %copy-done.2, f32[2,128,128]{2,1,0:T(8,128)} %probe.1, bf16[14,128,128]{2,1,0:T(8,128)(2,1)} %bitcast.14, s32[2,14]{1,0:T(2,128)} %bitcast.16, bf16[4,256,256]{2,1,0:T(8,128)(2,1)} %constant.18.clone.tables), custom_call_target="tpu_custom_call" | custom-call | tf_op jit(solution)/shard_map/middle/pallas_call | solution.py:191
  60.5 1.0 fusion
  61.4 2.9 %collective-permute-start.4 = (f32[32,896]{1,0:T(8,128)S(1)}, f32[32,896]{1,0:T(8,128)S(1)}, u32[]{:S(2)}, u32[]{:S(2)}) collective-permute-start(f32[32,896]{1,0:T(8,128)S(1)} %get-tuple-element.6), channel_id=1, source_target_pairs={{1,0},{2,1},{3,2},{4,3},{5,4},{6,5},{7,6},{8,7},{9,8},{10,9},{11,1... | collective-permute-start | bytes 344072 | tf_op jit(solution)/shard_map/ppermute | solution.py:212
  64.3 4.1 %collective-permute-start.5 = (f32[32,896]{1,0:T(8,128)S(1)}, f32[32,896]{1,0:T(8,128)S(1)}, u32[]{:S(2)}, u32[]{:S(2)}) collective-permute-start(f32[32,896]{1,0:T(8,128)S(1)} %get-tuple-element.7), channel_id=1, source_target_pairs={{0,1},{1,2},{2,3},{3,4},{4,5},{5,6},{6,7},{7,8},{8,9},{9,10},{10,1... | collective-permute-start | bytes 344072 | tf_op jit(solution)/shard_map/ppermute | solution.py:212
  68.4 0.9 fusion.1
  69.3 1.3 collective-permute-start.6
  70.6 4.1 %collective-permute-start.7 = (f32[24,896]{1,0:T(8,128)S(1)}, f32[24,896]{1,0:T(8,128)S(1)}, u32[]{:S(2)}, u32[]{:S(2)}) collective-permute-start(f32[24,896]{1,0:T(8,128)S(1)} %get-tuple-element.9), channel_id=1, source_target_pairs={{0,2},{1,3},{2,4},{3,5},{4,6},{5,7},{6,8},{7,9},{8,10},{9,11},{10,... | collective-permute-start | bytes 258056 | tf_op jit(solution)/shard_map/ppermute | solution.py:212
  74.8 1.8 collective-permute-done.7
  76.6 0.9 pad_add_fusion
  77.5 1.0 broadcast_in_dim.2
  78.5 10.1 %all-to-all-start.1 = ((f32[8,32,896]{2,1,0:T(8,128)}), f32[8,32,896]{2,1,0:T(8,128)S(1)}, u32[]{:S(2)}, u32[]{:S(2)}) async-start(f32[8,32,896]{2,1,0:T(8,128)} %broadcast_in_dim.2), calls=%async_computation.1 | async-start | bytes 1835008 | tf_op jit(solution)/shard_map/all_to_all | solution.py:229
  88.6 0.6 reduce_sum.32
  89.3 118.8 %psum.7 = f32[]{:T(128)} all-reduce(f32[]{:T(128)} %reduce_sum.32), channel_id=1, replica_groups=mesh['blk'=8,'wide'=64] {'blk','wide'}, use_global_device_ids=true, to_apply=%region_3.4 | all-reduce | flops 1 | bytes 8 | tf_op jit(solution)/shard_map/psum | solution.py:228
  208.3 0.7 bitcast_subtract_fusion
  (28 shorter events, 0.9 us)
Async XLA Ops:
  0.6 0.7 copy-start
  33.4 11.7 %collective-permute-start = (f32[24,896]{1,0:T(8,128)S(1)}, f32[24,896]{1,0:T(8,128)S(1)}, u32[]{:S(2)}, u32[]{:S(2)}) collective-permute-start(f32[24,896]{1,0:T(8,128)S(1)} %get-tuple-element.13), channel_id=1, source_target_pairs={{0,2},{1,3},{2,4},{3,5},{4,6},{5,7},{6,8},{7,9},{8,10},{9,11},{10,... | collective-permute-start | bytes 258056 | tf_op jit(solution)/shard_map/ppermute | solution.py:212
  36.6 8.5 %collective-permute-start.1 = (f32[32,896]{1,0:T(8,128)S(1)}, f32[32,896]{1,0:T(8,128)S(1)}, u32[]{:S(2)}, u32[]{:S(2)}) collective-permute-start(f32[32,896]{1,0:T(8,128)S(1)} %reduce_sum.29), channel_id=1, source_target_pairs={{0,1},{1,2},{2,3},{3,4},{4,5},{5,6},{6,7},{7,8},{8,9},{9,10},{10,1... | collective-permute-start | bytes 344072 | tf_op jit(solution)/shard_map/ppermute | solution.py:212
  41.8 6.1 %collective-permute-start.2 = (f32[32,896]{1,0:T(8,128)S(1)}, f32[32,896]{1,0:T(8,128)S(1)}, u32[]{:S(2)}, u32[]{:S(2)}) collective-permute-start(f32[32,896]{1,0:T(8,128)S(1)} %reduce_sum.29), channel_id=1, source_target_pairs={{1,0},{2,1},{3,2},{4,3},{5,4},{6,5},{7,6},{8,7},{9,8},{10,9},{11,1... | collective-permute-start | bytes 344072 | tf_op jit(solution)/shard_map/ppermute | solution.py:212
  43.8 5.9 %collective-permute-start.3 = (f32[24,896]{1,0:T(8,128)S(1)}, f32[24,896]{1,0:T(8,128)S(1)}, u32[]{:S(2)}, u32[]{:S(2)}) collective-permute-start(f32[24,896]{1,0:T(8,128)S(1)} %get-tuple-element.12), channel_id=1, source_target_pairs={{2,0},{3,1},{4,2},{5,3},{6,4},{7,5},{8,6},{9,7},{10,8},{11,9},{12,... | collective-permute-start | bytes 258056 | tf_op jit(solution)/shard_map/ppermute | solution.py:212
  49.6 0.8 copy-start.2
  61.4 15.2 %collective-permute-start.4 = (f32[32,896]{1,0:T(8,128)S(1)}, f32[32,896]{1,0:T(8,128)S(1)}, u32[]{:S(2)}, u32[]{:S(2)}) collective-permute-start(f32[32,896]{1,0:T(8,128)S(1)} %get-tuple-element.6), channel_id=1, source_target_pairs={{1,0},{2,1},{3,2},{4,3},{5,4},{6,5},{7,6},{8,7},{9,8},{10,9},{11,1... | collective-permute-start | bytes 344072 | tf_op jit(solution)/shard_map/ppermute | solution.py:212
  64.3 12.3 %collective-permute-start.5 = (f32[32,896]{1,0:T(8,128)S(1)}, f32[32,896]{1,0:T(8,128)S(1)}, u32[]{:S(2)}, u32[]{:S(2)}) collective-permute-start(f32[32,896]{1,0:T(8,128)S(1)} %get-tuple-element.7), channel_id=1, source_target_pairs={{0,1},{1,2},{2,3},{3,4},{4,5},{5,6},{6,7},{7,8},{8,9},{9,10},{10,1... | collective-permute-start | bytes 344072 | tf_op jit(solution)/shard_map/ppermute | solution.py:212
  69.3 5.5 %collective-permute-start.6 = (f32[24,896]{1,0:T(8,128)S(1)}, f32[24,896]{1,0:T(8,128)S(1)}, u32[]{:S(2)}, u32[]{:S(2)}) collective-permute-start(f32[24,896]{1,0:T(8,128)S(1)} %get-tuple-element.8), channel_id=1, source_target_pairs={{2,0},{3,1},{4,2},{5,3},{6,4},{7,5},{8,6},{9,7},{10,8},{11,9},{12,... | collective-permute-start | bytes 258056 | tf_op jit(solution)/shard_map/ppermute | solution.py:212
  70.6 5.9 %collective-permute-start.7 = (f32[24,896]{1,0:T(8,128)S(1)}, f32[24,896]{1,0:T(8,128)S(1)}, u32[]{:S(2)}, u32[]{:S(2)}) collective-permute-start(f32[24,896]{1,0:T(8,128)S(1)} %get-tuple-element.9), channel_id=1, source_target_pairs={{0,2},{1,3},{2,4},{3,5},{4,6},{5,7},{6,8},{7,9},{8,10},{9,11},{10,... | collective-permute-start | bytes 258056 | tf_op jit(solution)/shard_map/ppermute | solution.py:212
  78.5 10.1 %copy-start.4 = (f32[8]{0:T(128)S(1)}, f32[8]{0:T(128)}, u32[]{:S(2)}) copy-start(f32[8]{0:T(128)} %param.12) | copy-start | bytes 100
  78.5 10.1 %copy-start.3 = (f32[8,128]{1,0:T(8,128)S(1)}, f32[8,128]{1,0:T(8,128)}, u32[]{:S(2)}) copy-start(f32[8,128]{1,0:T(8,128)} %get-tuple-element.5) | copy-start | bytes 12292
  78.5 129.5 %all-to-all-start.1 = ((f32[8,32,896]{2,1,0:T(8,128)}), f32[8,32,896]{2,1,0:T(8,128)S(1)}, u32[]{:S(2)}, u32[]{:S(2)}) async-start(f32[8,32,896]{2,1,0:T(8,128)} %broadcast_in_dim.2), calls=%async_computation.1 | async-start | bytes 1835008 | tf_op jit(solution)/shard_map/all_to_all | solution.py:229
  88.6 119.7 %copy-start.1 = (f32[1,2,32,896]{3,2,1,0:T(8,128)S(1)}, f32[1,2,32,896]{3,2,1,0:T(8,128)}, u32[]{:S(2)}) copy-start(f32[1,2,32,896]{3,2,1,0:T(8,128)} %param.7) | copy-start | bytes 688132

commit v2 on v1

--- a/solution.py
+++ b/solution.py
@@ -15,6 +15,7 @@
 PCOLS = 14
 N_BLK = 8
 N_WIDE = 64
+MESH = pl.DeviceIdType.MESH
 TILES = COLS // 128
 FRAME = 144
 TOP = 56
@@ -67,25 +68,135 @@
     return [pl.ds(r, CHUNK) for r in range(0, PATCH, CHUNK)]
 
 
-def mid_kernel(phase, probe, measured, jitter, tables, grad, misfit, cosf, sinf, acc, probe2, wave, xs, vs, err):
+def fused_kernel(
+    volume, paths, steps, probe, measured, jitter, tables,
+    out, total,
+    xa, zs, zr, phase, cosf, sinf, acc, back, pair_g, ga, probe2, wave, xs, vs, err, mbuf,
+    send_sems, recv_sems,
+):
+    g = lax.axis_index("blk")
     w = lax.axis_index("wide")
+    x, zh = g // 2, g % 2
+    zl, y, core = w // 16, (w // 2) % 8, w % 2
+    z = zh * 4 + zl
+
+    def device(x_, y_, z_, core_):
+        return (x_ * 2 + z_ // 4, (z_ % 4) * 16 + y_ * 2 + core_)
+
+    x_up, x_down, x_far = (x + 1) % 4, (x + 3) % 4, (x + 2) % 4
+    ring = [(x_up * 2 + zh, w), (x_down * 2 + zh, w), (x_far * 2 + zh, w)]
+    across = (g + 1 - 2 * zh, w)
+    groups = (
+        (z, [device(x, y, (z + k) % 8, core) for k in range(1, 8)]),
+        (y, [device(x, (y + k) % 8, z, core) for k in range(1, 8)]),
+        (x * 2 + core, [device((x + k // 2) % 4, y, z, (core + k) % 2) for k in range(1, 8)]),
+    )
+    near = [(-1, w >= 1), (1, w < N_WIDE - 1), (-2, w >= 2), (2, w < N_WIDE - 2)]
+
+    counter = [0]
+    pending = []
+
+    def copy(src, dst, device_id, when=None):
+        k = counter[0]
+        counter[0] += 1
+        c = pltpu.make_async_remote_copy(
+            src_ref=src, dst_ref=dst, send_sem=send_sems.at[k], recv_sem=recv_sems.at[k],
+            device_id=device_id, device_id_type=MESH,
+        )
+        return c
+
+    def guarded(cond, f):
+        if cond is None:
+            f()
+        else:
+            pl.when(cond)(f)
+
+    def start(c, cond=None):
+        guarded(cond, c.start)
+        pending.append((c, cond))
+
+    def arrive(c, cond=None):
+        guarded(cond, c.wait_recv)
+
+    tile = [slice(c * 128, c * 128 + 128) for c in range(TILES)]
+    hop = [[copy(volume.at[:, :, tile[c]], xa.at[k, c], ring[k]) for k in range(3)] for c in range(TILES)]
+    cross = [copy(zs.at[c], zr.at[c], across) for c in range(TILES)]
+    rows_sent = {-1: (56, 32, 88), 1: (56, 32, 24), -2: (56, 24, 120), 2: (64, 24, 0)}
+    halo = [
+        [copy(phase.at[c, pl.ds(rows_sent[d][0], rows_sent[d][1]), :], phase.at[c, pl.ds(rows_sent[d][2], rows_sent[d][1]), :],
+              (g, jnp.clip(w + d, 0, N_WIDE - 1))) for d, _ in near]
+        for c in range(TILES)
+    ]
+    rows_back = {-1: (24, 32, 0), 1: (88, 32, 32), -2: (0, 24, 64), 2: (120, 24, 88)}
+    ret = [
+        [copy(acc.at[c + 1, pl.ds(rows_back[d][0], rows_back[d][1]), :], back.at[c, pl.ds(rows_back[d][2], rows_back[d][1]), :],
+              (g, jnp.clip(w + d, 0, N_WIDE - 1))) for d, _ in near]
+        for c in range(TILES)
+    ]
+    gcross = [copy(pair_g.at[c, 0], pair_g.at[c, 1], across) for c in range(TILES)]
+    ghop = [[[copy(pair_g.at[c, h], ga.at[k, c, h], ring[k]) for k in range(3)] for h in range(2)] for c in range(TILES)]
+    sums = [[copy(mbuf.at[s, groups[s][0]], mbuf.at[s, groups[s][0]], p) for p in groups[s][1]] for s in range(3)]
+
+    barrier = pltpu.get_barrier_semaphore()
+    for _, members in groups:
+        for p in members:
+            pl.semaphore_signal(barrier, inc=1, device_id=p, device_id_type=MESH)
+    for d, cond in near:
+        @pl.when(cond)
+        def _():
+            pl.semaphore_signal(barrier, inc=1, device_id=(g, jnp.clip(w + d, 0, N_WIDE - 1)), device_id_type=MESH)
+
+    init = jax.named_scope('init')
+    init.__enter__()
     probe2[:, :PATCH] = probe[...]
     probe2[:, PATCH:] = probe[...]
-    first = TOP - ROWS * w
-    for r in range(0, FRAME, 16):
-        row = lax.broadcasted_iota(jnp.int32, (16, COLS), 0) + r
-        inside = (row >= first) & (row < first + ROWS * N_WIDE)
-        co, si = cos_sin(phase[r : r + 16, :])
-        co = jnp.where(inside, co, 0.0)
-        si = jnp.where(inside, si, 0.0)
-        for t in range(TILES):
-            cosf[t + 1, r : r + 16, :] = co[:, t * 128 : t * 128 + 128]
-            sinf[t + 1, r : r + 16, :] = si[:, t * 128 : t * 128 + 128]
     for t in (0, TILES + 1):
         cosf[t] = jnp.zeros((FRAME, 128), F32)
         sinf[t] = jnp.zeros((FRAME, 128), F32)
     acc[...] = jnp.zeros(acc.shape, F32)
     err[...] = jnp.zeros(err.shape, F32)
+
+    init.__exit__(None, None, None)
+    neighbours = sum(cond.astype(jnp.int32) for _, cond in near)
+    with jax.named_scope('wait'):
+        pl.semaphore_wait(barrier, 21 + neighbours)
+
+    slabs = [g, x_down * 2 + zh, x_up * 2 + zh, x_far * 2 + zh]
+
+    def stage_b(c):
+        for k in range(3):
+            arrive(hop[c][k])
+        blocks = [(volume[l, :, tile[c]], xa[0, c, l], xa[1, c, l], xa[2, c, l]) for l in range(2)]
+
+        def term(angle):
+            s = jnp.zeros((ROWS, 128), F32)
+            for l in range(2):
+                for k in range(4):
+                    s = s + paths[angle, l, slabs[k]] * blocks[l][k]
+            return s
+
+        zs[c] = term(g + 1 - 2 * zh)
+        start(cross[c])
+        phase[c, TOP : TOP + ROWS, :] = term(g)
+
+    def stage_c(c):
+        arrive(cross[c])
+        phase[c, TOP : TOP + ROWS, :] = phase[c, TOP : TOP + ROWS, :] + zr[c]
+        for k, (d, cond) in enumerate(near):
+            start(halo[c][k], cond)
+
+    first = TOP - ROWS * w
+
+    def stage_d(c):
+        for k in (1, 0, 3, 2):
+            d = near[k][0]
+            arrive(halo[c][k], {1: w >= 1, -1: w < N_WIDE - 1, 2: w >= 2, -2: w < N_WIDE - 2}[d])
+        for r in range(0, FRAME, 24):
+            row = lax.broadcasted_iota(jnp.int32, (24, 128), 0) + r
+            inside = (row >= first) & (row < first + ROWS * N_WIDE)
+            co, si = cos_sin(jnp.where(inside, phase[c, r : r + 24, :], 0.0))
+            cosf[c + 1, r : r + 24, :] = jnp.where(inside, co, 0.0)
+            sinf[c + 1, r : r + 24, :] = jnp.where(inside, si, 0.0)
 
     def masks(pair, p):
         j = 2 * pair + p
@@ -172,64 +283,131 @@
         v = vs[slot]
         return mm(jnp.concatenate([th, th, tl], 1), jnp.concatenate([v, v[:256]], 0))
 
-    SLOTS = xs.shape[0]
-    if SLOTS == PCOLS // 2:
-        for pair in range(PCOLS // 2):
-            step(pair, pair)
-    else:
-        def loop(i, carry):
-            step(i, 0)
-            return carry
-        lax.fori_loop(0, PCOLS // 2, loop, 0)
-    for t in range(TILES):
-        grad[:, t * 128 : t * 128 + 128] = acc[t + 1]
-    misfit[...] = err[...]
-
-
-def middle(phase, probe, measured, jitter, slots=7):
+    def stage_e(pair):
+        step(pair, pair % 2)
+
+    def stage_f(c):
+        for k, (d, cond) in enumerate(near):
+            start(ret[c][k], cond)
+
+    def stage_g(c):
+        s = acc[c + 1, TOP : TOP + ROWS, :]
+        pair_g[c, 0] = s
+        for k, (d, cond) in enumerate(near):
+            ok = {1: w >= 1, -1: w < N_WIDE - 1, 2: w >= 2, -2: w < N_WIDE - 2}[d]
+            lo, n, at = {-1: (0, 32, 0), 1: (0, 32, 32), -2: (8, 24, 64), 2: (0, 24, 88)}[d]
+
+            @pl.when(ok)
+            def _():
+                ret[c][k].wait_recv()
+                pair_g[c, 0, lo : lo + n, :] = pair_g[c, 0, lo : lo + n, :] + back[c, at : at + n, :]
+
+        start(gcross[c])
+        for k in range(3):
+            start(ghop[c][0][k])
+
+    def stage_h(c):
+        arrive(gcross[c])
+        for k in range(3):
+            start(ghop[c][1][k])
+
+    angles = [g, g + 1 - 2 * zh, x_down * 2 + zh, x_down * 2 + 1 - zh, x_up * 2 + zh, x_up * 2 + 1 - zh, x_far * 2 + zh, x_far * 2 + 1 - zh]
+
+    def stage_j(c):
+        for k in range(3):
+            arrive(ghop[c][0][k])
+            arrive(ghop[c][1][k])
+        grads = [pair_g[c, 0], pair_g[c, 1], *(ga[k, c, h] for k in range(3) for h in range(2))]
+        for l in range(2):
+            s = jnp.zeros((ROWS, 128), F32)
+            for a, gr in zip(angles, grads):
+                s = s + (steps[a] * paths[a, l, g]) * gr
+            out[l, :, tile[c]] = s
+
+    def misfit_send(s, value):
+        mbuf[s, pl.ds(groups[s][0], 1)] = value[None]
+        for c in sums[s]:
+            start(c)
+
+    def misfit_take(s):
+        for c in sums[s]:
+            arrive(c)
+        v = mbuf[s, 0]
+        for k in range(1, 8):
+            v = v + mbuf[s, k]
+        return v
+
+    for c in range(TILES):
+        for k in range(3):
+            start(hop[c][k])
+
+    def stage_m(c):
+        value = misfit_take(c - 1) if c else err[...]
+        if c < 3:
+            misfit_send(c, value)
+        else:
+            total[0] = jnp.sum(value)
+
+    stages = dict(zip("BCDEFGHJM", (stage_b, stage_c, stage_d, stage_e, stage_f, stage_g, stage_h, stage_j, stage_m)))
+    for name, c in order():
+        with jax.named_scope(f"{name}{c}"):
+            stages[name](c)
+    for c, cond in pending:
+        guarded(cond, c.wait_send)
+
+
+DUE = dict(
+    B=(3.2, 1.4), C=(8.5, 1.4), D=(11.3, 1.4), E=(12.75, 1.55), F=(15.85, 1.55),
+    G=(19.0, 1.55), H=(24.5, 1.55), J=(28.1, 1.55), M=(23.7, 4.5),
+)
+
+
+def order():
+    due = []
+    for name, (begin, gap) in DUE.items():
+        for c in range(4 if name == "M" else TILES):
+            last = TILES - 2 if name == "F" else TILES
+            due.append((begin + gap * min(c, last), name, c))
+    return [(name, c) for _, name, c in sorted(due)]
+
+
+def fused(volume, paths, steps, probe, measured, jitter):
     vm = pl.BlockSpec(memory_space=pltpu.VMEM)
+    sm = pl.BlockSpec(memory_space=pltpu.SMEM)
+    copies = TILES * 19 + 21
+    grid = pltpu.VMEM((TILES + 2, FRAME, 128), F32)
     return pl.pallas_call(
-        mid_kernel,
-        out_shape=(jax.ShapeDtypeStruct((FRAME, COLS), F32), jax.ShapeDtypeStruct((8, 128), F32)),
-        in_specs=[vm, vm, vm, pl.BlockSpec(memory_space=pltpu.SMEM), vm],
-        out_specs=(vm, vm),
+        fused_kernel,
+        out_shape=(jax.ShapeDtypeStruct((2, ROWS, COLS), F32), jax.ShapeDtypeStruct((1,), F32)),
+        in_specs=[vm, sm, sm, vm, vm, sm, vm],
+        out_specs=(vm, sm),
         scratch_shapes=[
-            pltpu.VMEM((TILES + 2, FRAME, 128), F32),
-            pltpu.VMEM((TILES + 2, FRAME, 128), F32),
-            pltpu.VMEM((TILES + 2, FRAME, 128), F32),
+            pltpu.VMEM((3, TILES, 2, ROWS, 128), F32),
+            pltpu.VMEM((TILES, ROWS, 128), F32),
+            pltpu.VMEM((TILES, ROWS, 128), F32),
+            pltpu.VMEM((TILES, FRAME, 128), F32),
+            grid, grid, grid,
+            pltpu.VMEM((TILES, 112, 128), F32),
+            pltpu.VMEM((TILES, 2, ROWS, 128), F32),
+            pltpu.VMEM((3, TILES, 2, ROWS, 128), F32),
             pltpu.VMEM((2, 2 * PATCH, PATCH), F32),
-            pltpu.VMEM((slots, 2, 2, PATCH, PATCH), F32),
-            pltpu.VMEM((slots, 2 * PATCH, 512), BF16),
-            pltpu.VMEM((slots, 512, 2 * PATCH), BF16),
+            pltpu.VMEM((2, 2, 2, PATCH, PATCH), F32),
+            pltpu.VMEM((2, 2 * PATCH, 512), BF16),
+            pltpu.VMEM((2, 512, 2 * PATCH), BF16),
             pltpu.VMEM((8, 128), F32),
+            pltpu.VMEM((3, 8, 8, 128), F32),
+            pltpu.SemaphoreType.DMA((copies,)),
+            pltpu.SemaphoreType.DMA((copies,)),
         ],
-        name="middle",
-    )(phase, probe, measured, jitter, jnp.asarray(dft_tables()))
-
-
-def shifted(x, by):
-    pairs = [(i, i + by) for i in range(N_WIDE) if 0 <= i + by < N_WIDE]
-    return lax.ppermute(x, "wide", pairs)
+        compiler_params=pltpu.CompilerParams(collective_id=0, has_side_effects=True),
+        name="fused",
+    )(volume, paths, steps, probe, measured, jitter, jnp.asarray(dft_tables()))
 
 
 def body(volume, path_lengths, probe, measured, jitter, step_sizes):
-    group = lax.axis_index("blk")
-    slab = volume[0]
-    own = lax.dynamic_index_in_dim(path_lengths, group, 1, keepdims=False)
-    terms = own[:, 0, None, None] * slab[0] + own[:, 1, None, None] * slab[1]
-    proj = jnp.sum(lax.all_to_all(terms, "blk", 0, 0, tiled=True), 0)
-    frame = jnp.concatenate(
-        [shifted(proj[8:], 2), shifted(proj, 1), proj, shifted(proj, -1), shifted(proj[:24], -2)], 0
-    )
-    part, err = middle(frame, probe, measured[0, 0], jitter[:, 0, 0])
-    grad = part[56:88]
-    grad = grad + shifted(part[24:56], -1) + shifted(part[88:120], 1)
-    grad = grad + jnp.pad(shifted(part[:24], -2), ((8, 0), (0, 0))) + jnp.pad(shifted(part[120:], 2), ((0, 8), (0, 0)))
-    total = lax.psum(jnp.sum(err), ("blk", "wide"))
-    every = lax.all_to_all(jnp.broadcast_to(grad[None], (N_BLK, ROWS, COLS)), "blk", 0, 0, tiled=True)
-    coeffs = step_sizes[:, None] * own
-    update = jnp.sum(coeffs[:, :, None, None] * every[:, None], 0)
-    return (slab - update)[None], total
+    paths = jnp.transpose(path_lengths, (0, 2, 1))
+    update, total = fused(volume[0], paths, step_sizes, probe, measured[0, 0], jitter[:, 0, 0])
+    return volume - update[None], total[0]
 
 
 def solution(mesh):

time: 210 us -> 66.6 us (0.32)
  the two profiles are of different devices: /device:TPU:1 before, /device:TPU:6 now
where the time goes in v2:
time: 66.6 us; the launch traced here: 66.4 us
  Pallas kernels  62.4 us (94%)
  between operations  2.41 us (4%)
  other arithmetic  1.65 us (2%)
    pallas_call x1, Pallas kernels, fused(): pl.pallas_call(fused_kernel, out_shape=(jax.ShapeDtypeStruct((2, ROWS, CO...  62.4 us
    sub x1, other arithmetic, body(): return (volume - update[None], total[0])  1.65 us

profile of v2, /device:TPU:6, one launch (start us, length us, event | category | flops | bytes accessed | tf_op | source)
XLA Modules:
  0.0 66.4 jit_solution(2188350103362258643)
XLA Ops:
  0.6 0.0 copy-start
  0.6 62.4 %fused.1 = (f32[2,32,896]{2,1,0:T(8,128)}, f32[1]{0:T(128)}) custom-call(f32[2,32,896]{2,1,0:T(8,128)} %bitcast.7, f32[8,2,8]{2,1,0:T(2,128)} %bitcast.9, f32[8]{0:T(128)} %steps.1, f32[2,128,128]{2,1,0:T(8,128)} %probe.1, bf16[14,128,128]{2,1,0:T(8,128)(2,1)} %bitcast.8, s32[2,14]{1,0:T(2,128)} %bitcast.10, bf16[4,256,256]{2,1,0:T(8,128)(2,1)} %constant.2.clone.tables), custom_call_target="tpu_custom_call" | custom-call | tf_op jit(solution)/shard_map/fused/pallas_call | solution.py:379
  63.0 0.0 copy-done
  63.0 1.7 %bitcast_subtract_fusion = f32[1,2,32,896]{3,2,1,0:T(8,128)} fusion(f32[1,2,32,896]{3,2,1,0:T(8,128)S(1)} %copy-done, f32[2,32,896]{2,1,0:T(8,128)} %get-tuple-element.4), kind=kLoop, calls=%fused_computation | loop fusion | flops 57344 | bytes 688128 | tf_op jit(solution)/shard_map/sub | solution.py:410
Async XLA Ops:
  0.6 62.4 %copy-start = (f32[1,2,32,896]{3,2,1,0:T(8,128)S(1)}, f32[1,2,32,896]{3,2,1,0:T(8,128)}, u32[]{:S(2)}) copy-start(f32[1,2,32,896]{3,2,1,0:T(8,128)} %param.7) | copy-start | bytes 688132

commit v3 on v2

--- a/solution.py
+++ b/solution.py
@@ -69,8 +69,9 @@
 
 
 def fused_kernel(
-    volume, paths, steps, probe, measured, jitter, tables,
+    volume_in, paths_in, steps_in, probe_in, measured_in, jitter_in, tables_in,
     out, total,
+    volume, measured, tables, paths, steps, jitter, load_sems,
     xa, zs, zr, phase, cosf, sinf, acc, back, pair_g, ga, probe2, wave, xs, vs, err, mbuf,
     send_sems, recv_sems,
 ):
@@ -87,8 +88,8 @@
     ring = [(x_up * 2 + zh, w), (x_down * 2 + zh, w), (x_far * 2 + zh, w)]
     across = (g + 1 - 2 * zh, w)
     groups = (
+        (y, [device(x, (y + k) % 8, z, core) for k in range(1, 8)]),
         (z, [device(x, y, (z + k) % 8, core) for k in range(1, 8)]),
-        (y, [device(x, (y + k) % 8, z, core) for k in range(1, 8)]),
         (x * 2 + core, [device((x + k // 2) % 4, y, z, (core + k) % 2) for k in range(1, 8)]),
     )
     near = [(-1, w >= 1), (1, w < N_WIDE - 1), (-2, w >= 2), (2, w < N_WIDE - 2)]
@@ -137,6 +138,13 @@
     ghop = [[[copy(pair_g.at[c, h], ga.at[k, c, h], ring[k]) for k in range(3)] for h in range(2)] for c in range(TILES)]
     sums = [[copy(mbuf.at[s, groups[s][0]], mbuf.at[s, groups[s][0]], p) for p in groups[s][1]] for s in range(3)]
 
+    loads = [
+        pltpu.make_async_copy(src, dst, load_sems.at[k])
+        for k, (src, dst) in enumerate((
+            (volume_in, volume), (probe_in, probe2.at[:, pl.ds(0, PATCH)]), (probe_in, probe2.at[:, pl.ds(PATCH, PATCH)]),
+            (paths_in, paths), (steps_in, steps), (jitter_in, jitter), (measured_in, measured), (tables_in, tables),
+        ))
+    ]
     barrier = pltpu.get_barrier_semaphore()
     for _, members in groups:
         for p in members:
@@ -146,20 +154,23 @@
         def _():
             pl.semaphore_signal(barrier, inc=1, device_id=(g, jnp.clip(w + d, 0, N_WIDE - 1)), device_id_type=MESH)
 
-    init = jax.named_scope('init')
-    init.__enter__()
-    probe2[:, :PATCH] = probe[...]
-    probe2[:, PATCH:] = probe[...]
+    for c in loads:
+        c.start()
     for t in (0, TILES + 1):
         cosf[t] = jnp.zeros((FRAME, 128), F32)
         sinf[t] = jnp.zeros((FRAME, 128), F32)
     acc[...] = jnp.zeros(acc.shape, F32)
     err[...] = jnp.zeros(err.shape, F32)
 
-    init.__exit__(None, None, None)
     neighbours = sum(cond.astype(jnp.int32) for _, cond in near)
-    with jax.named_scope('wait'):
+    loads[0].wait()
+    with jax.named_scope("wait"):
         pl.semaphore_wait(barrier, 21 + neighbours)
+    for c in range(TILES):
+        for k in range(3):
+            start(hop[c][k])
+    for c in loads[1:]:
+        c.wait()
 
     slabs = [g, x_down * 2 + zh, x_up * 2 + zh, x_far * 2 + zh]
 
@@ -206,8 +217,30 @@
         row = lax.broadcasted_iota(jnp.int32, (16, PATCH), 0) >= jr
         return j, jr, s, lane, row
 
-    def step(pair, slot):
-        t1h, t1l, t2h, t2l = (tables[i] for i in range(4))
+    def put_rows(slot, p, c, a, b):
+        at = slice(p * PATCH + c, p * PATCH + c + CHUNK)
+        for k, x in enumerate((a, b)):
+            hi, lo = halves(x)
+            xs[slot, at, k * 128 : k * 128 + 128] = hi
+            xs[slot, at, 256 + k * 128 : 256 + k * 128 + 128] = lo
+
+    def right(slot, th, tl):
+        x = xs[slot]
+        return mm(jnp.concatenate([x, x[:, :256]], 1), jnp.concatenate([th, th, tl], 0))
+
+    def to_cols(slot, u):
+        for p in range(2):
+            for k in range(2):
+                for c in range(0, PATCH, CHUNK):
+                    hi, lo = halves(u[p * PATCH + c : p * PATCH + c + CHUNK, k * 128 : k * 128 + 128])
+                    vs[slot, k * PATCH + c : k * PATCH + c + CHUNK, p * 128 : p * 128 + 128] = hi
+                    vs[slot, 256 + k * PATCH + c : 256 + k * PATCH + c + CHUNK, p * 128 : p * 128 + 128] = lo
+
+    def left(slot, th, tl):
+        v = vs[slot]
+        return mm(jnp.concatenate([th, th, tl], 1), jnp.concatenate([v, v[:256]], 0))
+
+    def waves(pair, slot):
         for p in range(2):
             j, jr, s, lane, row = masks(pair, p)
             t = pair + p
@@ -230,8 +263,7 @@
                 wave[slot, p, 0, c : c + CHUNK, :] = w_r
                 wave[slot, p, 1, c : c + CHUNK, :] = w_i
                 put_rows(slot, p, c, w_r, w_i)
-        right_to_cols(slot, t1h, t1l)
-        y = left(slot, t2h, t2l)
+    def pointwise(pair, slot, y):
         e = err[...]
         for p in range(2):
             j = 2 * pair + p
@@ -245,10 +277,9 @@
                 for k in range(0, CHUNK, 8):
                     e = e + d2[k : k + 8]
                 ratio = target * lax.rsqrt(jnp.maximum(m2, 0.0625))
-                put_rows(slot, p, c, ratio * f_r, ratio * f_i)
+                put_rows(2 + slot, p, c, ratio * f_r, ratio * f_i)
         err[...] = e
-        right_to_cols(slot, t2h, t2l)
-        y = left(slot, t1h, t1l)
+    def accumulate(pair, slot, y):
         for p in range(2):
             j, jr, s, lane, row = masks(pair, p)
             t = pair + p
@@ -262,29 +293,24 @@
                         part = jnp.concatenate([jnp.where(row, part[:16], 0.0), part[16:]], 0)
                     acc[tile, c : c + CHUNK, :] += part
 
-    def put_rows(slot, p, c, a, b):
-        at = slice(p * PATCH + c, p * PATCH + c + CHUNK)
-        for k, x in enumerate((a, b)):
-            hi, lo = halves(x)
-            xs[slot, at, k * 128 : k * 128 + 128] = hi
-            xs[slot, at, 256 + k * 128 : 256 + k * 128 + 128] = lo
-
-    def right_to_cols(slot, th, tl):
-        x = xs[slot]
-        u = mm(jnp.concatenate([x, x[:, :256]], 1), jnp.concatenate([th, th, tl], 0))
-        for p in range(2):
-            for k in range(2):
-                for c in range(0, PATCH, CHUNK):
-                    hi, lo = halves(u[p * PATCH + c : p * PATCH + c + CHUNK, k * 128 : k * 128 + 128])
-                    vs[slot, k * PATCH + c : k * PATCH + c + CHUNK, p * 128 : p * 128 + 128] = hi
-                    vs[slot, 256 + k * PATCH + c : 256 + k * PATCH + c + CHUNK, p * 128 : p * 128 + 128] = lo
-
-    def left(slot, th, tl):
-        v = vs[slot]
-        return mm(jnp.concatenate([th, th, tl], 1), jnp.concatenate([v, v[:256]], 0))
-
-    def stage_e(pair):
-        step(pair, pair % 2)
+    def stage_e(i):
+        t1h, t1l, t2h, t2l = (tables[k] for k in range(4))
+        ahead, behind = i < PCOLS // 2, i > 0
+        if behind:
+            u2 = right(2 + (i - 1) % 2, t2h, t2l)
+        if ahead:
+            waves(i, i % 2)
+            u1 = right(i % 2, t1h, t1l)
+        if behind:
+            to_cols(1, u2)
+            y2 = left(1, t1h, t1l)
+        if ahead:
+            to_cols(0, u1)
+            y1 = left(0, t2h, t2l)
+        if behind:
+            accumulate(i - 1, (i - 1) % 2, y2)
+        if ahead:
+            pointwise(i, i % 2, y1)
 
     def stage_f(c):
         for k, (d, cond) in enumerate(near):
@@ -337,10 +363,6 @@
             v = v + mbuf[s, k]
         return v
 
-    for c in range(TILES):
-        for k in range(3):
-            start(hop[c][k])
-
     def stage_m(c):
         value = misfit_take(c - 1) if c else err[...]
         if c < 3:
@@ -356,32 +378,46 @@
         guarded(cond, c.wait_send)
 
 
-DUE = dict(
-    B=(3.2, 1.4), C=(8.5, 1.4), D=(11.3, 1.4), E=(12.75, 1.55), F=(15.85, 1.55),
-    G=(19.0, 1.55), H=(24.5, 1.55), J=(28.1, 1.55), M=(23.7, 4.5),
-)
+STEP = 1.0
 
 
 def order():
-    due = []
-    for name, (begin, gap) in DUE.items():
-        for c in range(4 if name == "M" else TILES):
-            last = TILES - 2 if name == "F" else TILES
-            due.append((begin + gap * min(c, last), name, c))
+    tiles = range(TILES)
+    due = [(2.2 + 1.4 * c, "B", c) for c in tiles] + [(8.1 + 1.4 * c, "C", c) for c in tiles]
+    ready = [11.6 + 1.4 * c for c in tiles]
+    due += [(t, "D", c) for c, t in enumerate(ready)]
+    done, now = [], 0.0
+    for i in range(TILES + 1):
+        now = max(now, ready[min(i + 1, TILES - 1)] + 0.01)
+        due.append((now, "E", i))
+        now += STEP
+        done.append(now - 0.01)
+    for c in tiles:
+        t = done[min(c + 2, TILES)]
+        due += [(t, "F", c), (t + 3.8 - 0.15 * c, "G", c), (t + 9.3 - 0.15 * c, "H", c), (t + 13.5 - 0.15 * c, "J", c)]
+    due += [(done[TILES - 1] - 0.001 + 4.6 * c, "M", c) for c in range(4)]
     return [(name, c) for _, name, c in sorted(due)]
 
 
 def fused(volume, paths, steps, probe, measured, jitter):
     vm = pl.BlockSpec(memory_space=pltpu.VMEM)
+    hbm = pl.BlockSpec(memory_space=pl.ANY)
     sm = pl.BlockSpec(memory_space=pltpu.SMEM)
     copies = TILES * 19 + 21
     grid = pltpu.VMEM((TILES + 2, FRAME, 128), F32)
     return pl.pallas_call(
         fused_kernel,
-        out_shape=(jax.ShapeDtypeStruct((2, ROWS, COLS), F32), jax.ShapeDtypeStruct((1,), F32)),
-        in_specs=[vm, sm, sm, vm, vm, sm, vm],
+        out_shape=(pltpu.VMEM((2, ROWS, COLS), F32), jax.ShapeDtypeStruct((1,), F32)),
+        in_specs=[hbm] * 7,
         out_specs=(vm, sm),
         scratch_shapes=[
+            pltpu.VMEM((2, ROWS, COLS), F32),
+            pltpu.VMEM((PCOLS, PATCH, PATCH), BF16),
+            pltpu.VMEM((4, 2 * PATCH, 2 * PATCH), BF16),
+            pltpu.SMEM((8, 2, 8), F32),
+            pltpu.SMEM((8,), F32),
+            pltpu.SMEM((2, PCOLS), jnp.int32),
+            pltpu.SemaphoreType.DMA((8,)),
             pltpu.VMEM((3, TILES, 2, ROWS, 128), F32),
             pltpu.VMEM((TILES, ROWS, 128), F32),
             pltpu.VMEM((TILES, ROWS, 128), F32),
@@ -392,7 +428,7 @@
             pltpu.VMEM((3, TILES, 2, ROWS, 128), F32),
             pltpu.VMEM((2, 2 * PATCH, PATCH), F32),
             pltpu.VMEM((2, 2, 2, PATCH, PATCH), F32),
-            pltpu.VMEM((2, 2 * PATCH, 512), BF16),
+            pltpu.VMEM((4, 2 * PATCH, 512), BF16),
             pltpu.VMEM((2, 512, 2 * PATCH), BF16),
             pltpu.VMEM((8, 128), F32),
             pltpu.VMEM((3, 8, 8, 128), F32),

time: 66.6 us -> 60.5 us (0.908)
  the two profiles are of different devices: /device:TPU:6 before, /device:TPU:1 now
where the time goes in v3:
time: 60.5 us; the launch traced here: 60.3 us
  Pallas kernels  57.2 us (95%)
  between operations  2.42 us (4%)
  other arithmetic  0.71 us (1%)
    pallas_call x1, Pallas kernels, fused(): pl.pallas_call(fused_kernel, out_shape=(pltpu.VMEM((2, ROWS, COLS), F32),...  57.2 us

profile of v3, /device:TPU:1, one launch (start us, length us, event | category | flops | bytes accessed | tf_op | source)
XLA Modules:
  0.0 60.3 jit_solution(1323686292208310015)
XLA Ops:
  0.6 0.0 copy-start
  0.6 57.2 %fused.1 = (f32[2,32,896]{2,1,0:T(8,128)S(1)}, f32[1]{0:T(128)}) custom-call(f32[2,32,896]{2,1,0:T(8,128)} %bitcast.7, f32[8,2,8]{2,1,0:T(2,128)} %bitcast.9, f32[8]{0:T(128)} %steps_in.1, f32[2,128,128]{2,1,0:T(8,128)} %probe_in.1, bf16[14,128,128]{2,1,0:T(8,128)(2,1)} %bitcast.8, s32[2,14]{1,0:T(2,128)} %bitcast.10, ...), custom_call_target="tpu_custom_call" | custom-call | tf_op jit(solution)/shard_map/fused/pallas_call | solution.py:408
  57.8 0.0 copy-done
  57.8 0.7 %bitcast_subtract_fusion = f32[1,2,32,896]{3,2,1,0:T(8,128)} fusion(f32[1,2,32,896]{3,2,1,0:T(8,128)S(1)} %copy-done, f32[2,32,896]{2,1,0:T(8,128)S(1)} %get-tuple-element.4), kind=kLoop, calls=%fused_computation | loop fusion | flops 57344 | bytes 688128 | tf_op jit(solution)/shard_map/sub | solution.py:446
Async XLA Ops:
  0.6 57.2 %copy-start = (f32[1,2,32,896]{3,2,1,0:T(8,128)S(1)}, f32[1,2,32,896]{3,2,1,0:T(8,128)}, u32[]{:S(2)}) copy-start(f32[1,2,32,896]{3,2,1,0:T(8,128)} %param.7) | copy-start | bytes 688132

commit v4 on v3

--- a/solution.py
+++ b/solution.py
@@ -72,7 +72,7 @@
     volume_in, paths_in, steps_in, probe_in, measured_in, jitter_in, tables_in,
     out, total,
     volume, measured, tables, paths, steps, jitter, load_sems,
-    xa, zs, zr, phase, cosf, sinf, acc, back, pair_g, ga, probe2, wave, xs, vs, err, mbuf,
+    xa, zv, xo, xi, zs, zr, phase, cosf, sinf, acc, back, pair_g, ga, probe2, wave, xs, vs, err, mbuf,
     send_sems, recv_sems,
 ):
     g = lax.axis_index("blk")
@@ -97,14 +97,33 @@
     counter = [0]
     pending = []
 
-    def copy(src, dst, device_id, when=None):
-        k = counter[0]
-        counter[0] += 1
-        c = pltpu.make_async_remote_copy(
-            src_ref=src, dst_ref=dst, send_sem=send_sems.at[k], recv_sem=recv_sems.at[k],
-            device_id=device_id, device_id_type=MESH,
-        )
-        return c
+    class Group:
+        def __init__(self, moves, totals):
+            k = counter[0]
+            counter[0] += 1
+
+            def describe(src, dst, device_id):
+                return pltpu.make_async_remote_copy(
+                    src_ref=src, dst_ref=dst, send_sem=send_sems.at[k], recv_sem=recv_sems.at[k],
+                    device_id=device_id, device_id_type=MESH,
+                )
+
+            self.moves = [describe(*m) for m in moves]
+            self.totals = [(describe(ref, ref, ring[0]), cond) for ref, cond in totals]
+
+        def start(self, which=None, conds=None):
+            for k in range(len(self.moves)) if which is None else which:
+                guarded(conds[k] if conds else None, self.moves[k].start)
+            if self not in pending:
+                pending.append(self)
+
+        def arrive(self):
+            for c, cond in self.totals:
+                guarded(cond, c.wait_recv)
+
+        def sent(self):
+            for c, cond in self.totals:
+                guarded(cond, c.wait_send)
 
     def guarded(cond, f):
         if cond is None:
@@ -112,31 +131,40 @@
         else:
             pl.when(cond)(f)
 
-    def start(c, cond=None):
-        guarded(cond, c.start)
-        pending.append((c, cond))
-
-    def arrive(c, cond=None):
-        guarded(cond, c.wait_recv)
+    near_conds = [cond for _, cond in near]
+    at_end = (w == 0) | (w == N_WIDE - 1)
+    by_end = (w == 1) | (w == N_WIDE - 2)
+    inner = (w > 1) & (w < N_WIDE - 2)
+
+    def near_group(moves, c):
+        return Group(moves, [(back.at[c, pl.ds(0, n)], cond) for n, cond in ((112, inner), (88, by_end), (56, at_end))])
 
     tile = [slice(c * 128, c * 128 + 128) for c in range(TILES)]
-    hop = [[copy(volume.at[:, :, tile[c]], xa.at[k, c], ring[k]) for k in range(3)] for c in range(TILES)]
-    cross = [copy(zs.at[c], zr.at[c], across) for c in range(TILES)]
+    hop = {
+        c: Group([(volume.at[:, :, tile[c]], xa.at[k, c], ring[k]) for k in range(3)], [(xa.at[:, c], None)])
+        for c in range(TILES) if c not in Z_FIRST
+    }
+    raw = {c: Group([(volume.at[:, :, tile[c]], zv.at[c], across)], [(zv.at[c], None)]) for c in Z_FIRST}
+    spread = {c: Group([(xo.at[c, k], xi.at[c, k], ring[k]) for k in range(3)], [(xi.at[c], None)]) for c in Z_FIRST}
+    cross = {c: Group([(zs.at[c], zr.at[c], across)], [(zr.at[c], None)]) for c in range(TILES) if c not in Z_FIRST}
     rows_sent = {-1: (56, 32, 88), 1: (56, 32, 24), -2: (56, 24, 120), 2: (64, 24, 0)}
     halo = [
-        [copy(phase.at[c, pl.ds(rows_sent[d][0], rows_sent[d][1]), :], phase.at[c, pl.ds(rows_sent[d][2], rows_sent[d][1]), :],
-              (g, jnp.clip(w + d, 0, N_WIDE - 1))) for d, _ in near]
+        near_group([(phase.at[c, pl.ds(rows_sent[d][0], rows_sent[d][1]), :], phase.at[c, pl.ds(rows_sent[d][2], rows_sent[d][1]), :],
+                     (g, jnp.clip(w + d, 0, N_WIDE - 1))) for d, _ in near], c)
         for c in range(TILES)
     ]
     rows_back = {-1: (24, 32, 0), 1: (88, 32, 32), -2: (0, 24, 64), 2: (120, 24, 88)}
     ret = [
-        [copy(acc.at[c + 1, pl.ds(rows_back[d][0], rows_back[d][1]), :], back.at[c, pl.ds(rows_back[d][2], rows_back[d][1]), :],
-              (g, jnp.clip(w + d, 0, N_WIDE - 1))) for d, _ in near]
+        near_group([(acc.at[c + 1, pl.ds(rows_back[d][0], rows_back[d][1]), :], back.at[c, pl.ds(rows_back[d][2], rows_back[d][1]), :],
+                     (g, jnp.clip(w + d, 0, N_WIDE - 1))) for d, _ in near], c)
         for c in range(TILES)
     ]
-    gcross = [copy(pair_g.at[c, 0], pair_g.at[c, 1], across) for c in range(TILES)]
-    ghop = [[[copy(pair_g.at[c, h], ga.at[k, c, h], ring[k]) for k in range(3)] for h in range(2)] for c in range(TILES)]
-    sums = [[copy(mbuf.at[s, groups[s][0]], mbuf.at[s, groups[s][0]], p) for p in groups[s][1]] for s in range(3)]
+    gcross = [Group([(pair_g.at[c, 0], pair_g.at[c, 1], across)], [(zr.at[c], None)]) for c in range(TILES)]
+    ghop = [
+        Group([(pair_g.at[c, h], ga.at[k, c, h], ring[k]) for h in range(2) for k in range(3)], [(ga.at[:, c], None)])
+        for c in range(TILES)
+    ]
+    sums = [Group([(mbuf.at[s, groups[s][0]], mbuf.at[s, groups[s][0]], p) for p in groups[s][1]], [(mbuf.at[s, pl.ds(0, 7)], None)]) for s in range(3)]
 
     loads = [
         pltpu.make_async_copy(src, dst, load_sems.at[k])
@@ -166,17 +194,35 @@
     loads[0].wait()
     with jax.named_scope("wait"):
         pl.semaphore_wait(barrier, 21 + neighbours)
-    for c in range(TILES):
-        for k in range(3):
-            start(hop[c][k])
+    for c in Z_FIRST:
+        raw[c].start()
+    for c in hop:
+        hop[c].start()
     for c in loads[1:]:
         c.wait()
 
     slabs = [g, x_down * 2 + zh, x_up * 2 + zh, x_far * 2 + zh]
 
+    partner = g + 1 - 2 * zh
+
+    def stage_b_across(c):
+        raw[c].arrive()
+
+        def both(angle):
+            s = jnp.zeros((ROWS, 128), F32)
+            for l in range(2):
+                s = s + paths[angle, l, g] * volume[l, :, tile[c]] + paths[angle, l, partner] * zv[c, l]
+            return s
+
+        for k, x_ in enumerate((x_up, x_down, x_far)):
+            xo[c, k] = both(x_ * 2 + zh)
+            spread[c].start([k])
+        phase[c, TOP : TOP + ROWS, :] = both(g)
+
     def stage_b(c):
-        for k in range(3):
-            arrive(hop[c][k])
+        if c in Z_FIRST:
+            return stage_b_across(c)
+        hop[c].arrive()
         blocks = [(volume[l, :, tile[c]], xa[0, c, l], xa[1, c, l], xa[2, c, l]) for l in range(2)]
 
         def term(angle):
@@ -187,21 +233,23 @@
             return s
 
         zs[c] = term(g + 1 - 2 * zh)
-        start(cross[c])
+        cross[c].start()
         phase[c, TOP : TOP + ROWS, :] = term(g)
 
     def stage_c(c):
-        arrive(cross[c])
-        phase[c, TOP : TOP + ROWS, :] = phase[c, TOP : TOP + ROWS, :] + zr[c]
-        for k, (d, cond) in enumerate(near):
-            start(halo[c][k], cond)
+        if c in Z_FIRST:
+            spread[c].arrive()
+            rest = xi[c, 0] + xi[c, 1] + xi[c, 2]
+        else:
+            cross[c].arrive()
+            rest = zr[c]
+        phase[c, TOP : TOP + ROWS, :] = phase[c, TOP : TOP + ROWS, :] + rest
+        halo[c].start(conds=near_conds)
 
     first = TOP - ROWS * w
 
     def stage_d(c):
-        for k in (1, 0, 3, 2):
-            d = near[k][0]
-            arrive(halo[c][k], {1: w >= 1, -1: w < N_WIDE - 1, 2: w >= 2, -2: w < N_WIDE - 2}[d])
+        halo[c].arrive()
         for r in range(0, FRAME, 24):
             row = lax.broadcasted_iota(jnp.int32, (24, 128), 0) + r
             inside = (row >= first) & (row < first + ROWS * N_WIDE)
@@ -313,36 +361,30 @@
             pointwise(i, i % 2, y1)
 
     def stage_f(c):
-        for k, (d, cond) in enumerate(near):
-            start(ret[c][k], cond)
+        ret[c].start(conds=near_conds)
 
     def stage_g(c):
-        s = acc[c + 1, TOP : TOP + ROWS, :]
-        pair_g[c, 0] = s
+        pair_g[c, 0] = acc[c + 1, TOP : TOP + ROWS, :]
+        ret[c].arrive()
         for k, (d, cond) in enumerate(near):
             ok = {1: w >= 1, -1: w < N_WIDE - 1, 2: w >= 2, -2: w < N_WIDE - 2}[d]
             lo, n, at = {-1: (0, 32, 0), 1: (0, 32, 32), -2: (8, 24, 64), 2: (0, 24, 88)}[d]
 
             @pl.when(ok)
             def _():
-                ret[c][k].wait_recv()
                 pair_g[c, 0, lo : lo + n, :] = pair_g[c, 0, lo : lo + n, :] + back[c, at : at + n, :]
 
-        start(gcross[c])
-        for k in range(3):
-            start(ghop[c][0][k])
+        gcross[c].start()
+        ghop[c].start((0, 1, 2))
 
     def stage_h(c):
-        arrive(gcross[c])
-        for k in range(3):
-            start(ghop[c][1][k])
+        gcross[c].arrive()
+        ghop[c].start((3, 4, 5))
 
     angles = [g, g + 1 - 2 * zh, x_down * 2 + zh, x_down * 2 + 1 - zh, x_up * 2 + zh, x_up * 2 + 1 - zh, x_far * 2 + zh, x_far * 2 + 1 - zh]
 
     def stage_j(c):
-        for k in range(3):
-            arrive(ghop[c][0][k])
-            arrive(ghop[c][1][k])
+        ghop[c].arrive()
         grads = [pair_g[c, 0], pair_g[c, 1], *(ga[k, c, h] for k in range(3) for h in range(2))]
         for l in range(2):
             s = jnp.zeros((ROWS, 128), F32)
@@ -352,12 +394,10 @@
 
     def misfit_send(s, value):
         mbuf[s, pl.ds(groups[s][0], 1)] = value[None]
-        for c in sums[s]:
-            start(c)
+        sums[s].start()
 
     def misfit_take(s):
-        for c in sums[s]:
-            arrive(c)
+        sums[s].arrive()
         v = mbuf[s, 0]
         for k in range(1, 8):
             v = v + mbuf[s, k]
@@ -371,31 +411,47 @@
             total[0] = jnp.sum(value)
 
     stages = dict(zip("BCDEFGHJM", (stage_b, stage_c, stage_d, stage_e, stage_f, stage_g, stage_h, stage_j, stage_m)))
-    for name, c in order():
+    def drop(count):
+        for c in pending[:count]:
+            c.sent()
+        del pending[:count]
+
+    plan = order()
+    tail = plan.index(("F", TILES - 1)) + 1
+    for at, (name, c) in enumerate(plan):
+        if at >= tail and len(pending) > 9:
+            drop(3)
         with jax.named_scope(f"{name}{c}"):
             stages[name](c)
-    for c, cond in pending:
-        guarded(cond, c.wait_send)
+    with jax.named_scope("end"):
+        drop(len(pending))
 
 
 STEP = 1.0
+Z_FIRST = (1, 2)
 
 
 def order():
     tiles = range(TILES)
-    due = [(2.2 + 1.4 * c, "B", c) for c in tiles] + [(8.1 + 1.4 * c, "C", c) for c in tiles]
-    ready = [11.6 + 1.4 * c for c in tiles]
-    due += [(t, "D", c) for c, t in enumerate(ready)]
+    due, ready, turn = [], [], {True: 0, False: 0}
+    for c in tiles:
+        z_first = c in Z_FIRST
+        k = turn[z_first]
+        turn[z_first] += 1
+        begin = 6.9 + 1.4 * k if z_first else 2.2 + 1.4 * k
+        joined = begin + (2.7 if z_first else 6.6)
+        due += [(begin, "B", c), (joined, "C", c), (joined + 3.7, "D", c)]
+        ready.append(joined + 3.7)
     done, now = [], 0.0
     for i in range(TILES + 1):
-        now = max(now, ready[min(i + 1, TILES - 1)] + 0.01)
+        now = max(now, max(ready[: i + 2]) + 0.01)
         due.append((now, "E", i))
         now += STEP
         done.append(now - 0.01)
     for c in tiles:
         t = done[min(c + 2, TILES)]
         due += [(t, "F", c), (t + 3.8 - 0.15 * c, "G", c), (t + 9.3 - 0.15 * c, "H", c), (t + 13.5 - 0.15 * c, "J", c)]
-    due += [(done[TILES - 1] - 0.001 + 4.6 * c, "M", c) for c in range(4)]
+    due += [(done[TILES - 1] - 0.001 + t, "M", c) for c, t in enumerate((0.0, 4.6, 10.4, 15.0))]
     return [(name, c) for _, name, c in sorted(due)]
 
 
@@ -403,7 +459,7 @@
     vm = pl.BlockSpec(memory_space=pltpu.VMEM)
     hbm = pl.BlockSpec(memory_space=pl.ANY)
     sm = pl.BlockSpec(memory_space=pltpu.SMEM)
-    copies = TILES * 19 + 21
+    copies = TILES * 6 + 3
     grid = pltpu.VMEM((TILES + 2, FRAME, 128), F32)
     return pl.pallas_call(
         fused_kernel,
@@ -419,6 +475,9 @@
             pltpu.SMEM((2, PCOLS), jnp.int32),
             pltpu.SemaphoreType.DMA((8,)),
             pltpu.VMEM((3, TILES, 2, ROWS, 128), F32),
+            pltpu.VMEM((TILES, 2, ROWS, 128), F32),
+            pltpu.VMEM((TILES, 3, ROWS, 128), F32),
+            pltpu.VMEM((TILES, 3, ROWS, 128), F32),
             pltpu.VMEM((TILES, ROWS, 128), F32),
             pltpu.VMEM((TILES, ROWS, 128), F32),
             pltpu.VMEM((TILES, FRAME, 128), F32),

time: 60.5 us -> 57.5 us (0.950)
  Pallas kernels: 57.2 us -> 54.2 us
    pallas_call x1, Pallas kernels: 57.2 us -> 54.2 us  [fused(): pl.pallas_call(fused_kernel, out_shape=(pltpu.VMEM((2, ROWS, COLS), F32),...]
where the time goes in v4:
time: 57.5 us; the launch traced here: 57.4 us
  Pallas kernels  54.2 us (94%)
  between operations  2.42 us (4%)
  other arithmetic  0.71 us (1%)
    pallas_call x1, Pallas kernels, fused(): pl.pallas_call(fused_kernel, out_shape=(pltpu.VMEM((2, ROWS, COLS), F32),...  54.2 us

profile of v4, /device:TPU:1, one launch (start us, length us, event | category | flops | bytes accessed | tf_op | source)
XLA Modules:
  0.0 57.4 jit_solution(14495350133336647970)
XLA Ops:
  0.6 0.0 copy-start
  0.6 54.2 %fused.1 = (f32[2,32,896]{2,1,0:T(8,128)S(1)}, f32[1]{0:T(128)}) custom-call(f32[2,32,896]{2,1,0:T(8,128)} %bitcast.7, f32[8,2,8]{2,1,0:T(2,128)} %bitcast.9, f32[8]{0:T(128)} %steps_in.1, f32[2,128,128]{2,1,0:T(8,128)} %probe_in.1, bf16[14,128,128]{2,1,0:T(8,128)(2,1)} %bitcast.8, s32[2,14]{1,0:T(2,128)} %bitcast.10, ...), custom_call_target="tpu_custom_call" | custom-call | tf_op jit(solution)/shard_map/fused/pallas_call | solution.py:464
  54.9 0.0 copy-done
  54.9 0.7 %bitcast_subtract_fusion = f32[1,2,32,896]{3,2,1,0:T(8,128)} fusion(f32[1,2,32,896]{3,2,1,0:T(8,128)S(1)} %copy-done, f32[2,32,896]{2,1,0:T(8,128)S(1)} %get-tuple-element.4), kind=kLoop, calls=%fused_computation | loop fusion | flops 57344 | bytes 688128 | tf_op jit(solution)/shard_map/sub | solution.py:505
Async XLA Ops:
  0.6 54.3 %copy-start = (f32[1,2,32,896]{3,2,1,0:T(8,128)S(1)}, f32[1,2,32,896]{3,2,1,0:T(8,128)}, u32[]{:S(2)}) copy-start(f32[1,2,32,896]{3,2,1,0:T(8,128)} %param.7) | copy-start | bytes 688132

commit v5 on v4

--- a/solution.py
+++ b/solution.py
@@ -408,7 +408,7 @@
         if c < 3:
             misfit_send(c, value)
         else:
-            total[0] = jnp.sum(value)
+            total[...] = jnp.full((8, 128), jnp.sum(value), F32)
 
     stages = dict(zip("BCDEFGHJM", (stage_b, stage_c, stage_d, stage_e, stage_f, stage_g, stage_h, stage_j, stage_m)))
     def drop(count):
@@ -458,14 +458,13 @@
 def fused(volume, paths, steps, probe, measured, jitter):
     vm = pl.BlockSpec(memory_space=pltpu.VMEM)
     hbm = pl.BlockSpec(memory_space=pl.ANY)
-    sm = pl.BlockSpec(memory_space=pltpu.SMEM)
     copies = TILES * 6 + 3
     grid = pltpu.VMEM((TILES + 2, FRAME, 128), F32)
     return pl.pallas_call(
         fused_kernel,
-        out_shape=(pltpu.VMEM((2, ROWS, COLS), F32), jax.ShapeDtypeStruct((1,), F32)),
+        out_shape=(pltpu.VMEM((2, ROWS, COLS), F32), pltpu.VMEM((8, 128), F32)),
         in_specs=[hbm] * 7,
-        out_specs=(vm, sm),
+        out_specs=(vm, vm),
         scratch_shapes=[
             pltpu.VMEM((2, ROWS, COLS), F32),
             pltpu.VMEM((PCOLS, PATCH, PATCH), BF16),
@@ -502,7 +501,7 @@
 def body(volume, path_lengths, probe, measured, jitter, step_sizes):
     paths = jnp.transpose(path_lengths, (0, 2, 1))
     update, total = fused(volume[0], paths, step_sizes, probe, measured[0, 0], jitter[:, 0, 0])
-    return volume - update[None], total[0]
+    return volume - update[None], total[0, 0]
 
 
 def solution(mesh):

time: 57.5 us -> 55.8 us (0.970)
  between operations: 2.42 us -> 0.65 us
where the time goes in v5:
time: 55.8 us; the launch traced here: 55.6 us
  Pallas kernels  53.7 us (96%)
  other arithmetic  0.72 us (1%)
  between operations  0.65 us (1%)
    pallas_call x1, Pallas kernels, fused(): pl.pallas_call(fused_kernel, out_shape=(pltpu.VMEM((2, ROWS, COLS), F32),...  53.7 us

profile of v5, /device:TPU:1, one launch (start us, length us, event | category | flops | bytes accessed | tf_op | source)
XLA Modules:
  0.0 55.6 jit_solution(5883811169327174246)
XLA Ops:
  0.6 0.0 copy-start
  0.6 53.7 %fused.1 = (f32[2,32,896]{2,1,0:T(8,128)S(1)}, f32[8,128]{1,0:T(8,128)S(1)}) custom-call(f32[2,32,896]{2,1,0:T(8,128)} %bitcast.7, f32[8,2,8]{2,1,0:T(2,128)} %bitcast.9, f32[8]{0:T(128)} %steps_in.1, f32[2,128,128]{2,1,0:T(8,128)} %probe_in.1, bf16[14,128,128]{2,1,0:T(8,128)(2,1)} %bitcast.8, s32[2,14]{1,0:T(2,128)} %bitcast.10, ...), custom_call_target="tpu_custom_call" | custom-call | tf_op jit(solution)/shard_map/fused/pallas_call | solution.py:463
  54.4 0.5 slice.3
  54.9 0.0 copy-done
  54.9 0.7 %bitcast_subtract_fusion = f32[1,2,32,896]{3,2,1,0:T(8,128)} fusion(f32[1,2,32,896]{3,2,1,0:T(8,128)S(1)} %copy-done, f32[2,32,896]{2,1,0:T(8,128)S(1)} %get-tuple-element.4), kind=kLoop, calls=%fused_computation | loop fusion | flops 57344 | bytes 688128 | tf_op jit(solution)/shard_map/sub | solution.py:504
Async XLA Ops:
  0.6 54.3 %copy-start = (f32[1,2,32,896]{3,2,1,0:T(8,128)S(1)}, f32[1,2,32,896]{3,2,1,0:T(8,128)}, u32[]{:S(2)}) copy-start(f32[1,2,32,896]{3,2,1,0:T(8,128)} %param.7) | copy-start | bytes 688132

commit v6 on v5

--- a/solution.py
+++ b/solution.py
@@ -404,7 +404,7 @@
         return v
 
     def stage_m(c):
-        value = misfit_take(c - 1) if c else err[...]
+        value = misfit_take(c - 1) if c else jnp.sum(err[...], 0, keepdims=True)
         if c < 3:
             misfit_send(c, value)
         else:
@@ -489,7 +489,7 @@
             pltpu.VMEM((4, 2 * PATCH, 512), BF16),
             pltpu.VMEM((2, 512, 2 * PATCH), BF16),
             pltpu.VMEM((8, 128), F32),
-            pltpu.VMEM((3, 8, 8, 128), F32),
+            pltpu.VMEM((3, 8, 1, 128), F32),
             pltpu.SemaphoreType.DMA((copies,)),
             pltpu.SemaphoreType.DMA((copies,)),
         ],

time: 55.8 us -> 54.8 us (0.982)
  Pallas kernels: 53.7 us -> 52.8 us
    pallas_call x1, Pallas kernels: 53.7 us -> 52.8 us  [fused(): pl.pallas_call(fused_kernel, out_shape=(pltpu.VMEM((2, ROWS, COLS), F32),...]
where the time goes in v6:
time: 54.8 us; the launch traced here: 54.7 us
  Pallas kernels  52.8 us (96%)
  other arithmetic  0.72 us (1%)
  between operations  0.65 us (1%)
    pallas_call x1, Pallas kernels, fused(): pl.pallas_call(fused_kernel, out_shape=(pltpu.VMEM((2, ROWS, COLS), F32),...  52.8 us

profile of v6, /device:TPU:1, one launch (start us, length us, event | category | flops | bytes accessed | tf_op | source)
XLA Modules:
  0.0 54.7 jit_solution(16013495895459146704)
XLA Ops:
  0.6 0.0 copy-start
  0.6 52.8 %fused.1 = (f32[2,32,896]{2,1,0:T(8,128)S(1)}, f32[8,128]{1,0:T(8,128)S(1)}) custom-call(f32[2,32,896]{2,1,0:T(8,128)} %bitcast.7, f32[8,2,8]{2,1,0:T(2,128)} %bitcast.9, f32[8]{0:T(128)} %steps_in.1, f32[2,128,128]{2,1,0:T(8,128)} %probe_in.1, bf16[14,128,128]{2,1,0:T(8,128)(2,1)} %bitcast.8, s32[2,14]{1,0:T(2,128)} %bitcast.10, ...), custom_call_target="tpu_custom_call" | custom-call | tf_op jit(solution)/shard_map/fused/pallas_call | solution.py:463
  53.4 0.5 slice.3
  54.0 0.0 copy-done
  54.0 0.7 %bitcast_subtract_fusion = f32[1,2,32,896]{3,2,1,0:T(8,128)} fusion(f32[1,2,32,896]{3,2,1,0:T(8,128)S(1)} %copy-done, f32[2,32,896]{2,1,0:T(8,128)S(1)} %get-tuple-element.4), kind=kLoop, calls=%fused_computation | loop fusion | flops 57344 | bytes 688128 | tf_op jit(solution)/shard_map/sub | solution.py:504
Async XLA Ops:
  0.6 53.3 %copy-start = (f32[1,2,32,896]{3,2,1,0:T(8,128)S(1)}, f32[1,2,32,896]{3,2,1,0:T(8,128)}, u32[]{:S(2)}) copy-start(f32[1,2,32,896]{3,2,1,0:T(8,128)} %param.7) | copy-start | bytes 688132
